TPU v7x, 256 devices: a 8x8x2 block of a 8x8x16 slice. The times are simulated.
256 devices in a mesh: ga: 2 (over z), aa: 64 (over y, x), ba: 2 (over core).
Axes of the slice: x: 8, y: 8, z: 2, core: 2. Of those that a mesh axis runs over, the one named last changes fastest.
The devices are a block of a 8x8x16 slice.
Arguments:
- images: bfloat16 [16384, 12, 4096], P(('ga', 'aa', 'ba')), parts along dimension 0, may hold values from -6 to 6
- key_projection: bfloat16 [4096, 512], replicated, may hold values from -0.09375 to 0.09375
- value_projection: bfloat16 [4096, 512], replicated, may hold values from -0.09375 to 0.09375
- key_norm_gain: float32 [128], replicated, may hold values from 0.1 to 1.9
- hidden: bfloat16 [16384, 4096], P(('ga', 'aa'), 'ba'), parts along dimension 0, may hold values from -6 to 6
- shared_query_base: bfloat16 [16384, 2048], P(('ga', 'aa'), 'ba'), parts along dimension 0, may hold values from -220 to 220
- adapter_down_matrix: bfloat16 [64, 4096, 16], P('aa'), may hold values from -0.09375 to 0.09375
- adapter_up_matrix: bfloat16 [64, 16, 2048], P('aa'), may hold values from -1.5 to 1.5
- tenant_adapter_index: int32 [16384, 1], P(('ga', 'aa')), parts along dimension 0, may hold values from 0 to 63; in each aligned block of 128 rows (0 to 127, 128 to 255, ...) at most 4 rows name the same one
- used_tile_count: int32 [16384], P(('ga', 'aa', 'ba')), parts along dimension 0, may hold values from 1 to 4
Outputs:
- attended: bfloat16 [16384, 2048], P(('ga', 'aa', 'ba')), parts along dimension 0
There are 2 independent parts, one for each index of `ga`. A program takes and returns all parts, laid end to end along the dimension named above; an argument that names none is the same for every part. Nothing has to cross between parts.
Inputs may be any that keep to these rules, and one draw needn't show every extreme that they name: `tenant_adapter_index`: among the 128 requests of one index of aa (aligned blocks) no adapter is named more than 4 times.
All inputs are finite; a program needn't handle non-finite values.
Results may differ from a plain program's by a relative error of at most 0.012.
The roundings to bfloat16 on the way count: a program that leaves them out, or rounds other values in their place, can miss the bound.
Values may be sent and summed in bfloat16 or wider, within the bound.
No kernel may reach another device: no remote copies, remote signals or barrier semaphores. Data moves between devices by JAX's collectives and lax.ppermute only.
A program may use at most 128 MiB of HBM per device.

v0:
```python
import math

import jax
import jax.numpy as jnp
from jax import lax
from jax.sharding import PartitionSpec as P

TILE_TOKENS = 3


def copy_for_each(value, axis):
    peers = lax.axis_size(axis)
    return lax.all_to_all(
        jnp.broadcast_to(value[None], (peers, *value.shape)), axis, 0, 0, tiled=True
    )


def taken_together(value, axis):
    return copy_for_each(value, axis).sum(axis=0)


def on_device(
    images,
    key_projection,
    value_projection,
    key_norm_gain,
    hidden,
    shared_query_base,
    adapter_down_matrix,
    adapter_up_matrix,
    tenant_adapter_index,
    used_tile_count,
):
    requests = hidden.shape[0]
    half_model = hidden.shape[1]
    half_query = shared_query_base.shape[1]
    head_size = key_norm_gain.shape[0]
    heads_kv = key_projection.shape[1] // head_size
    bank_count = lax.axis_size("aa")
    slots_most = 2 * requests // bank_count
    our_side = lax.axis_index("ba")
    owner_ids = tenant_adapter_index[:, 0]
    owner_hot = (owner_ids[:, None] == jnp.arange(bank_count, dtype=jnp.int32)[None, :]).astype(
        jnp.float32
    )
    lower_ones = (jnp.arange(requests)[:, None] > jnp.arange(requests)[None, :]).astype(
        jnp.bfloat16
    )
    before = jnp.dot(lower_ones, owner_hot.astype(jnp.bfloat16), preferred_element_type=jnp.float32)
    rank_in = jnp.sum(before * owner_hot, axis=1)
    slot_hot = (rank_in[:, None] == jnp.arange(slots_most, dtype=jnp.float32)[None, :]).astype(
        jnp.float32
    )
    placing = (
        (owner_hot[:, :, None] * slot_hot[:, None, :])
        .reshape(requests, bank_count * slots_most)
        .astype(jnp.bfloat16)
    )
    down_half = lax.dynamic_slice_in_dim(
        adapter_down_matrix[0], our_side * half_model, half_model, 0
    )
    up_half = lax.dynamic_slice_in_dim(adapter_up_matrix[0], our_side * half_query, half_query, 1)
    packed = lax.dot_general(
        placing, hidden, (((0,), (0,)), ((), ())), preferred_element_type=jnp.float32
    )
    received_rows = lax.all_to_all(
        packed.astype(jnp.bfloat16).reshape(bank_count, slots_most, hidden.shape[1]),
        "aa",
        split_axis=0,
        concat_axis=0,
        tiled=True,
    )
    low_part = jnp.dot(
        received_rows.reshape(-1, half_model), down_half, preferred_element_type=jnp.float32
    )
    reduced_rank_part = taken_together(low_part, "ba")
    raised_output = jnp.dot(
        reduced_rank_part.astype(jnp.bfloat16), up_half, preferred_element_type=jnp.float32
    )
    raised_output = raised_output.astype(jnp.bfloat16).reshape(
        received_rows.shape[0], received_rows.shape[1], half_query
    )
    returned = lax.all_to_all(raised_output, "aa", split_axis=0, concat_axis=0, tiled=True)
    flat_back = returned.reshape(bank_count * slots_most, returned.shape[2])
    delta_half = jnp.dot(placing, flat_back, preferred_element_type=jnp.float32)
    query_half = (shared_query_base.astype(jnp.float32) + delta_half).astype(jnp.bfloat16)
    query_rows = lax.all_to_all(query_half, "ba", split_axis=0, concat_axis=1, tiled=True)
    requests_here = images.shape[0]
    local_rows = images.shape[1]
    flattened_rows = images.reshape(requests_here * local_rows, images.shape[2])
    unnormed_keys = jnp.dot(
        flattened_rows, key_projection, preferred_element_type=jnp.float32
    ).reshape(requests_here, local_rows, heads_kv, head_size)
    key_scale = lax.rsqrt(jnp.mean(unnormed_keys * unnormed_keys, axis=-1, keepdims=True) + 1e-06)
    keys_local = (unnormed_keys * key_scale * key_norm_gain).astype(jnp.bfloat16)
    values_local = jnp.dot(
        flattened_rows, value_projection, preferred_element_type=jnp.float32
    ).astype(jnp.bfloat16)
    values_local = values_local.reshape(requests_here, local_rows, heads_kv, head_size)
    query_group_width = query_rows.shape[1] // (heads_kv * head_size)
    query_four_axes = query_rows.reshape(requests_here, heads_kv, query_group_width, head_size)
    scores = jnp.einsum(
        "rkgd,rjkd->rkgj", query_four_axes, keys_local, preferred_element_type=jnp.float32
    ) / math.sqrt(head_size)
    position = jnp.arange(local_rows, dtype=jnp.int32) // TILE_TOKENS
    valid_rows = position[None, :] < used_tile_count[:, None]
    key_mask = valid_rows[:, None, None, :]
    masked = jnp.where(key_mask, scores, -1e30)
    score_peak = jnp.max(masked, axis=-1)
    weights = jnp.where(key_mask, jnp.exp(masked - score_peak[..., None]), 0.0)
    weight_total = jnp.sum(weights, axis=-1)
    weighted = jnp.einsum(
        "rkgj,rjkd->rkgd",
        weights.astype(jnp.bfloat16),
        values_local,
        preferred_element_type=jnp.float32,
    )
    attended = (weighted / weight_total[..., None]).reshape(requests_here, -1).astype(jnp.bfloat16)
    return attended


def solution(mesh):
    placed = (
        P(("ga", "aa", "ba"), None, None),
        P(),
        P(),
        P(),
        P(("ga", "aa"), "ba"),
        P(("ga", "aa"), "ba"),
        P("aa", None, None),
        P("aa", None, None),
        P(("ga", "aa"), None),
        P(("ga", "aa", "ba")),
    )
    return jax.shard_map(
        on_device,
        mesh=mesh,
        in_specs=placed,
        out_specs=P(("ga", "aa", "ba"), None),
        check_vma=False,
    )
```

profile of v0, /device:TPU:513, one launch (start us, length us, event | category | flops | bytes accessed | tf_op | source)
XLA Modules:
  0.0 111.0 jit_solution(15379478204448119320)
XLA Ops:
  0.0 0.0 copy-start
  0.0 0.9 fusion.10
  0.9 0.7 fusion.21
  1.6 0.0 copy-done
  1.6 0.4 convolution_convert_fusion
  2.1 1.2 %reshape.126 = bf16[64,4,2048]{2,1,0:T(4,128)(2,1)} reshape(bf16[256,2048]{1,0:T(8,128)(2,1)S(1)} %convolution_convert_fusion) | data formatting | bytes 2097152 | tf_op jit(solution)/shard_map/reshape | solution.py:67
  3.3 21.8 %all-to-all-start = ((bf16[64,4,2048]{2,1,0:T(4,128)(2,1)}), bf16[64,4,2048]{2,1,0:T(4,128)(2,1)S(1)}, u32[]{:S(2)}, u32[]{:S(2)}) async-start(bf16[64,4,2048]{2,1,0:T(4,128)(2,1)} %reshape.126), calls=%async_computation | async-start | bytes 2097152 | tf_op jit(solution)/shard_map/all_to_all | solution.py:66
  25.1 9.6 %copy.35 = bf16[64,12,4096]{2,1,0:T(8,128)(2,1)} copy(bf16[64,12,4096]{2,0,1:T(8,128)(2,1)} %param.10) | data formatting | bytes 12582912 | tf_op args[0]
  34.7 9.9 %reshape.130 = bf16[768,4096]{1,0:T(8,128)(2,1)} reshape(bf16[64,12,4096]{2,1,0:T(8,128)(2,1)} %copy.35) | data formatting | bytes 12582912 | tf_op jit(solution)/shard_map/reshape | solution.py:90
  44.6 6.4 %copy.38 = bf16[512,4096]{1,0:T(8,128)(2,1)} copy(bf16[512,4096]{0,1:T(8,128)(2,1)} %bitcast.36) | data formatting | bytes 8388608 | tf_op jit(solution)/shard_map/dot_general | solution.py:91
  51.0 0.0 copy-start.2
  51.0 0.0 copy-start.3
  51.0 7.9 %multiply_reduce_fusion = (f32[64,12,4]{0,2,1:T(4,128)S(1)}, f32[64,12,4,128]{3,0,2,1:T(8,128)}) fusion(bf16[4,128,4096,1]{2,1,0,3:T(8,128)(2,1)} %bitcast.37, bf16[64,12,4096]{2,0,1:T(8,128)(2,1)} %param.10), kind=kOutput, calls=%fused_computation.5 | convolution fusion | flops 3222008832 | bytes 12070912 | tf_op jit(solution)/shard_map/dot_general | solution.py:91
  58.9 0.0 all-to-all-done
  58.9 0.3 reshape.127
  59.2 0.0 copy-done.2
  59.2 0.4 fusion.15
  59.6 8.5 %all_to_all.31 = f32[2,256,16]{1,2,0:T(8,128)S(1)} all-to-all(f32[2,256,16]{1,2,0:T(8,128)S(1)} %broadcast_in_dim.17), channel_id=1, replica_groups=mesh['ga'=2,'aa'=64,'ba'=2] {'ba'}, dimensions={0} | all-to-all | bytes 65536 | tf_op jit(solution)/shard_map/all_to_all | solution.py:13
  68.1 0.0 copy-done.3
  68.1 0.3 convolution_convert_fusion.2
  68.5 1.0 reshape.128
  69.5 13.6 %all-to-all-start.2 = ((bf16[64,4,1024]{2,1,0:T(4,128)(2,1)}), bf16[64,4,1024]{2,1,0:T(4,128)(2,1)S(1)}, u32[]{:S(2)}, u32[]{:S(2)}) async-start(bf16[64,4,1024]{2,1,0:T(4,128)(2,1)} %reshape.128), calls=%async_computation.2 | async-start | bytes 1048576 | tf_op jit(solution)/shard_map/all_to_all | solution.py:83
  83.1 0.0 copy-start.4
  83.1 0.0 copy-start.1
  83.1 0.0 copy-start.5
  83.1 8.4 %convolution_convert_fusion.1 = bf16[768,512]{1,0:T(8,128)(2,1)} fusion(bf16[768,4096]{1,0:T(8,128)(2,1)} %reshape.130, bf16[4096,512]{1,0:T(8,128)(2,1)} %param.12), kind=kOutput, calls=%fused_computation.6 | convolution fusion | flops 3221618688 | bytes 11272192 | tf_op jit(solution)/shard_map/dot_general | solution.py:96
  91.5 1.7 %reshape.131 = bf16[64,12,4,128]{3,2,1,0:T(4,128)(2,1)S(1)} reshape(bf16[768,512]{1,0:T(8,128)(2,1)} %convolution_convert_fusion.1) | data formatting | bytes 1572864 | tf_op jit(solution)/shard_map/reshape | solution.py:99
  93.3 0.0 copy-done.4
  93.3 0.1 broadcast_compare_fusion
  93.4 0.0 copy-done.1
  93.4 0.0 copy-done.5
  93.4 1.4 %multiply_convert_fusion = bf16[64,12,4,128]{3,0,2,1:T(8,128)(2,1)} fusion(f32[64,12,4,128]{3,0,2,1:T(8,128)S(1)} %copy-done.1, f32[128]{0:T(128)S(1)} %copy-done.5, f32[64,12,4]{0,2,1:T(4,128)S(1)} %add_rsqrt_fusion), kind=kLoop, calls=%fused_computation.4 | loop fusion | flops 1179648 | bytes 2372096 | tf_op jit(solution)/shard_map/convert_element_type | solution.py:95
  94.8 4.4 %all-to-all-done.2 = bf16[64,4,1024]{2,1,0:T(4,128)(2,1)S(1)} async-done(((bf16[64,4,1024]{2,1,0:T(4,128)(2,1)}), bf16[64,4,1024]{2,1,0:T(4,128)(2,1)S(1)}, u32[]{:S(2)}, u32[]{:S(2)}) %all-to-all-start.2) | async-done | bytes 524320 | tf_op jit(solution)/shard_map/all_to_all | solution.py:83
  99.2 1.3 %fusion.9 = bf16[128,1024]{1,0:T(8,128)(2,1)S(1)} fusion(bf16[64,4,1024]{2,1,0:T(4,128)(2,1)S(1)} %all-to-all-done.2, bf16[128,1024]{1,0:T(8,128)(2,1)} %param.15, bf16[128,64,4]{0,2,1:T(4,128)(2,1)S(1)} %multiply_convert_fusion.1), kind=kOutput, calls=%fused_computation.17 | convolution fusion | flops 67502080 | bytes 1114112 | tf_op jit(solution)/shard_map/dot_general | solution.py:85
  100.5 6.4 %all_to_all.32 = bf16[2,64,1024]{2,1,0:T(8,128)(2,1)S(1)} all-to-all(bf16[2,64,1024]{2,1,0:T(8,128)(2,1)S(1)} %bitcast.38), channel_id=1, replica_groups=mesh['ga'=2,'aa'=64,'ba'=2] {'ba'}, dimensions={0} | all-to-all | bytes 524288 | tf_op jit(solution)/shard_map/all_to_all | solution.py:87
  106.8 0.3 copy.32
  107.1 0.2 reshape.129
  107.3 2.3 %fusion.28 = (f32[64,4,4]{2,1,0:T(4,128)S(1)}, bf16[64,4,4,12]{3,2,1,0:T(4,128)(2,1)S(1)}) fusion(pred[64,12]{1,0:T(8,128)(4,1)S(1)} %broadcast_compare_fusion, bf16[64,4,4,128]{3,2,1,0:T(4,128)(2,1)S(1)} %reshape.129, bf16[64,12,4,128]{3,0,2,1:T(8,128)(2,1)} %multiply_convert_fusion), kind=kOutput, calls=%fused_computation.46 | convolution fusion | flops 3219467 | bytes 1078016 | tf_op jit(solution)/shard_map/sub | solution.py:110
  109.6 0.5 fusion.8
  110.1 0.9 convert_element_type.69
  (6 shorter events, 0.1 us)
Async XLA Ops:
  0.0 1.6 %copy-start = (bf16[128,2048]{1,0:T(8,128)(2,1)S(1)}, bf16[128,2048]{1,0:T(8,128)(2,1)}, u32[]{:S(2)}) copy-start(bf16[128,2048]{1,0:T(8,128)(2,1)} %param.14) | copy-start | bytes 1572868
  3.3 55.6 %all-to-all-start = ((bf16[64,4,2048]{2,1,0:T(4,128)(2,1)}), bf16[64,4,2048]{2,1,0:T(4,128)(2,1)S(1)}, u32[]{:S(2)}, u32[]{:S(2)}) async-start(bf16[64,4,2048]{2,1,0:T(4,128)(2,1)} %reshape.126), calls=%async_computation | async-start | bytes 2097152 | tf_op jit(solution)/shard_map/all_to_all | solution.py:66
  51.0 8.2 %copy-start.2 = (bf16[1,4096,16]{1,2,0:T(8,128)(2,1)S(1)}, bf16[1,4096,16]{1,2,0:T(8,128)(2,1)}, u32[]{:S(2)}) copy-start(bf16[1,4096,16]{1,2,0:T(8,128)(2,1)} %param.16) | copy-start | bytes 393220
  51.0 17.2 %copy-start.3 = (bf16[1,16,2048]{2,1,0:T(8,128)(2,1)S(1)}, bf16[1,16,2048]{2,1,0:T(8,128)(2,1)}, u32[]{:S(2)}) copy-start(bf16[1,16,2048]{2,1,0:T(8,128)(2,1)} %param.17) | copy-start | bytes 196612
  69.5 29.7 %all-to-all-start.2 = ((bf16[64,4,1024]{2,1,0:T(4,128)(2,1)}), bf16[64,4,1024]{2,1,0:T(4,128)(2,1)S(1)}, u32[]{:S(2)}, u32[]{:S(2)}) async-start(bf16[64,4,1024]{2,1,0:T(4,128)(2,1)} %reshape.128), calls=%async_computation.2 | async-start | bytes 1048576 | tf_op jit(solution)/shard_map/all_to_all | solution.py:83
  83.1 10.2 %copy-start.4 = (s32[64]{0:T(128)S(1)}, s32[64]{0:T(128)}, u32[]{:S(2)}) copy-start(s32[64]{0:T(128)} %param.19) | copy-start | bytes 772
  83.1 10.3 %copy-start.1 = (f32[64,12,4,128]{3,0,2,1:T(8,128)S(1)}, f32[64,12,4,128]{3,0,2,1:T(8,128)}, u32[]{:S(2)}) copy-start(f32[64,12,4,128]{3,0,2,1:T(8,128)} %get-tuple-element.6) | copy-start | bytes 4718596
  83.1 10.3 %copy-start.5 = (f32[128]{0:T(128)S(1)}, f32[128]{0:T(128)}, u32[]{:S(2)}) copy-start(f32[128]{0:T(128)} %param.13) | copy-start | bytes 1540
where the time goes:
time: 112 us; the launch traced here: 111 us
  starting transfers between devices  35.4 us (32%)
  local copies, waits for them, and re-layouts  31.5 us (28%)
  matrix products  22.4 us (20%)
  blocking collectives  14.9 us (13%)
  waiting for transfers between devices  4.39 us (4%)
  other arithmetic  2.17 us (2%)
    all_to_all x1, starting transfers between devices, on_device(): lax.all_to_all(packed.astype(jnp.bfloat16).reshape(bank_count, slots_most...  21.8 us
    all_to_all x1, starting transfers between devices, on_device(): lax.all_to_all(raised_output, 'aa', split_axis=0, concat_axis=0, tiled=True)  13.6 us
    reshape x1, local copies, waits for them, and re-layouts, on_device(): flattened_rows = images.reshape(requests_here * local_rows, images.shape[2])  9.85 us
    unnamed x13, local copies, waits for them, and re-layouts  9.64 us
    all_to_all x1, blocking collectives, copy_for_each(): lax.all_to_all(jnp.broadcast_to(value[None], (peers, *value.shape)), axis...  8.54 us
    dot_general x1, matrix products, on_device(): jnp.dot(flattened_rows, value_projection, preferred_element_type=jnp.floa...  8.41 us
    dot_general x1, matrix products, on_device(): jnp.dot(flattened_rows, key_projection, preferred_element_type=jnp.float32)  7.94 us
    dot_general x1, local copies, waits for them, and re-layouts, on_device(): jnp.dot(flattened_rows, key_projection, preferred_element_type=jnp.float32)  6.41 us
  transfers between devices with their start and end apart: 2, of which 1 were waited for; matrix products, arithmetic and copies ran while one was open for 41% of the time, Pallas kernels for 0%

commit v1 on v0

v1 whole, which is shorter than its diff:
```python
import functools
import math

import jax
import jax.numpy as jnp
from jax import lax
from jax.experimental import pallas as pl
from jax.experimental.pallas import tpu as pltpu
from jax.sharding import PartitionSpec as P

TILE_TOKENS = 3
CHUNK = 16
SLOTS = 4


def project_kernel(heads, size, x_ref, wk_ref, wv_ref, gain_ref, keys_ref, values_ref):
    x = x_ref[...]
    raw = jnp.dot(x, wk_ref[...], preferred_element_type=jnp.float32)
    for h in range(heads):
        part = raw[:, h * size : (h + 1) * size]
        scale = lax.rsqrt(jnp.mean(part * part, axis=-1, keepdims=True) + 1e-06)
        keys_ref[:, h * size : (h + 1) * size] = (part * scale * gain_ref[...]).astype(jnp.bfloat16)
    values_ref[...] = jnp.dot(x, wv_ref[...], preferred_element_type=jnp.float32).astype(jnp.bfloat16)


def project(x, wk, wv, gain):
    rows, width = x.shape
    kvw = wk.shape[1]
    size = gain.shape[1]
    tile = rows // 6 if rows % 6 == 0 and (rows // 6) % 16 == 0 else rows
    whole = lambda i: (0, 0)
    return pl.pallas_call(
        functools.partial(project_kernel, kvw // size, size),
        grid=(rows // tile,),
        in_specs=[
            pl.BlockSpec((tile, width), lambda i: (i, 0)),
            pl.BlockSpec((width, kvw), whole),
            pl.BlockSpec((width, kvw), whole),
            pl.BlockSpec((1, size), whole),
        ],
        out_specs=[pl.BlockSpec((tile, kvw), lambda i: (i, 0))] * 2,
        out_shape=[jax.ShapeDtypeStruct((rows, kvw), jnp.bfloat16)] * 2,
        cost_estimate=pl.CostEstimate(
            flops=4 * rows * width * kvw,
            bytes_accessed=2 * (rows * width + 2 * width * kvw + 2 * rows * kvw),
            transcendentals=0,
        ),
        name="project",
    )(x, wk, wv, gain)


def attend_kernel(requests, tokens, heads, group, size, q_ref, k_ref, v_ref, valid_ref, out_ref):
    wide = tokens * CHUNK
    row = lax.broadcasted_iota(jnp.int32, (group * CHUNK, wide), 0)
    col = lax.broadcasted_iota(jnp.int32, (group * CHUNK, wide), 1)
    same = (row % CHUNK) == (col % CHUNK)
    for c in range(requests // CHUNK):
        rows = slice(c * CHUNK, (c + 1) * CHUNK)
        use = same & (valid_ref[c : c + 1, :] > 0.0)
        for h in range(heads):
            lanes = slice(h * size, (h + 1) * size)
            q = jnp.concatenate(
                [
                    q_ref[rows, (h * group + g) * size : (h * group + g + 1) * size]
                    for g in range(group)
                ],
                axis=0,
            )
            k = k_ref[:, rows, lanes].reshape(wide, size)
            v = v_ref[:, rows, lanes].reshape(wide, size)
            scores = lax.dot_general(
                q, k, (((1,), (1,)), ((), ())), preferred_element_type=jnp.float32
            ) / math.sqrt(size)
            scores = jnp.where(use, scores, -jnp.inf)
            weights = jnp.exp(scores - jnp.max(scores, axis=-1, keepdims=True))
            total = jnp.sum(weights, axis=-1, keepdims=True)
            weighted = jnp.dot(weights.astype(jnp.bfloat16), v, preferred_element_type=jnp.float32)
            done = (weighted / total).astype(jnp.bfloat16)
            for g in range(group):
                out_ref[rows, (h * group + g) * size : (h * group + g + 1) * size] = done[
                    g * CHUNK : (g + 1) * CHUNK
                ]


def attend(q, keys, values, valid, size):
    tokens, requests, kvw = keys.shape
    heads = kvw // size
    group = q.shape[1] // kvw
    return pl.pallas_call(
        functools.partial(attend_kernel, requests, tokens, heads, group, size),
        out_shape=jax.ShapeDtypeStruct(q.shape, jnp.bfloat16),
        in_specs=[pl.BlockSpec(memory_space=pltpu.VMEM)] * 4,
        out_specs=pl.BlockSpec(memory_space=pltpu.VMEM),
        cost_estimate=pl.CostEstimate(
            flops=4 * q.size * tokens * CHUNK,
            bytes_accessed=4 * q.size + 4 * keys.size,
            transcendentals=0,
        ),
        name="attend",
    )(q, keys, values, valid)


def on_device(
    images,
    key_projection,
    value_projection,
    key_norm_gain,
    hidden,
    shared_query_base,
    adapter_down_matrix,
    adapter_up_matrix,
    tenant_adapter_index,
    used_tile_count,
):
    requests, half_model = hidden.shape
    half_query = shared_query_base.shape[1]
    size = key_norm_gain.shape[0]
    banks = lax.axis_size("aa")
    swap = [(0, 1), (1, 0)]
    ours = lax.axis_index("ba")

    owner = tenant_adapter_index[:, 0]
    hot = owner[:, None] == jnp.arange(banks, dtype=jnp.int32)[None, :]
    lower = jnp.arange(requests)[:, None] > jnp.arange(requests)[None, :]
    before = jnp.dot(
        lower.astype(jnp.bfloat16), hot.astype(jnp.bfloat16), preferred_element_type=jnp.float32
    )
    place = jnp.sum(jnp.where(hot, before, 0.0), axis=1).astype(jnp.int32)
    slots = banks * SLOTS
    slot = owner * SLOTS + place
    placing = (slot[:, None] == jnp.arange(slots, dtype=jnp.int32)[None, :]).astype(jnp.bfloat16)

    packed = lax.dot_general(
        placing, hidden, (((0,), (0,)), ((), ())), preferred_element_type=jnp.float32
    ).astype(jnp.bfloat16)
    rows_in = lax.all_to_all(
        packed.reshape(banks, SLOTS, half_model), "aa", 0, 0, tiled=True
    ).reshape(slots, half_model)

    down = lax.dynamic_slice_in_dim(
        adapter_down_matrix[0].T, ours * half_model, half_model, 1
    )
    up = lax.dynamic_slice_in_dim(adapter_up_matrix[0], ours * half_query, half_query, 1)

    here, tokens, width = images.shape
    x = images.transpose(1, 0, 2).reshape(tokens * here, width)
    keys, values = project(x, key_projection, value_projection, key_norm_gain[None, :])

    low = lax.dot_general(
        rows_in, down, (((1,), (1,)), ((), ())), preferred_element_type=jnp.float32
    )
    low = low + lax.ppermute(low, "ba", swap)
    raised = jnp.dot(low.astype(jnp.bfloat16), up, preferred_element_type=jnp.float32).astype(
        jnp.bfloat16
    )
    back = lax.all_to_all(
        raised.reshape(banks, SLOTS, half_query), "aa", 0, 0, tiled=True
    ).reshape(slots, half_query)
    delta = jnp.dot(placing, back, preferred_element_type=jnp.float32)
    query = (shared_query_base.astype(jnp.float32) + delta).astype(jnp.bfloat16)
    kept = lax.dynamic_slice_in_dim(query, ours * here, here, 0)
    sent = lax.dynamic_slice_in_dim(query, (1 - ours) * here, here, 0)
    got = lax.ppermute(sent, "ba", swap)
    first = jnp.where(ours == 0, kept, got)
    second = jnp.where(ours == 0, got, kept)
    q = jnp.concatenate([first, second], axis=1)

    position = jnp.arange(tokens, dtype=jnp.int32) // TILE_TOKENS
    valid = position[None, :, None] < used_tile_count.reshape(here // CHUNK, 1, CHUNK)
    valid = valid.astype(jnp.float32).reshape(here // CHUNK, tokens * CHUNK)
    return attend(
        q,
        keys.reshape(tokens, here, -1),
        values.reshape(tokens, here, -1),
        valid,
        size,
    )


def solution(mesh):
    placed = (
        P(("ga", "aa", "ba"), None, None),
        P(),
        P(),
        P(),
        P(("ga", "aa"), "ba"),
        P(("ga", "aa"), "ba"),
        P("aa", None, None),
        P("aa", None, None),
        P(("ga", "aa"), None),
        P(("ga", "aa", "ba")),
    )
    return jax.shard_map(
        on_device,
        mesh=mesh,
        in_specs=placed,
        out_specs=P(("ga", "aa", "ba"), None),
        check_vma=False,
    )
```

time: 112 us -> 93.5 us (0.83)
  local copies, waits for them, and re-layouts: 31.5 us -> 2.94 us
  waiting for transfers between devices: 4.39 us -> 27.1 us
  matrix products: 22.4 us -> 2.41 us
  Pallas kernels: 0 us -> 18.5 us
  blocking collectives: 14.9 us -> 0 us
  starting transfers between devices: 35.4 us -> 39.9 us
    all_to_all x2, waiting for transfers between devices: 4.39 us -> 25.9 us  [the longest x1 22.1 us: on_device(): lax.all_to_all(packed.reshape(banks, SLOTS, half_model), 'aa', 0, 0, tile...]
    pallas_call x0 -> x2, Pallas kernels: none -> 18.5 us  [the longest x1 12.2 us: project(): pl.pallas_call(functools.partial(project_kernel, kvw // size, size), grid...]
    dot_general x7 -> x4, matrix products: 19.7 us -> 1.86 us  [the longest x1 0.9 us: on_device(): jnp.dot(lower.astype(jnp.bfloat16), hot.astype(jnp.bfloat16), preferred_e...]
    all_to_all x2 -> x0, blocking collectives: 14.9 us -> none  [the longest x1 8.54 us: copy_for_each(): lax.all_to_all(jnp.broadcast_to(value[None], (peers, *value.shape)), axis...]
    reshape x6 -> x4, local copies, waits for them, and re-layouts: 14.3 us -> 2.58 us  [the longest x1 1.2 us: on_device(): packed.reshape(banks, SLOTS, half_model)]
    ppermute x0 -> x2, starting transfers between devices: none -> 10.3 us  [the longest x1 7.4 us: on_device(): low = low + lax.ppermute(low, 'ba', swap)]
    unnamed x13 -> x10, local copies, waits for them, and re-layouts: 9.64 us -> 0.02 us
    dot_general x1 -> x0, local copies, waits for them, and re-layouts: 6.41 us -> none  [on_device(): jnp.dot(flattened_rows, key_projection, preferred_element_type=jnp.float32)]
  transfers between devices with their start and end apart: 2 -> 4, of which waited for: 1 -> 4; matrix products, arithmetic and copies ran while one was open for 41% -> 1% of each run, Pallas kernels for 0% -> 13%
where the time goes in v1:
time: 93.5 us; the launch traced here: 93.1 us
  starting transfers between devices  39.9 us (43%)
  waiting for transfers between devices  27.1 us (29%)
  Pallas kernels  18.5 us (20%)
  local copies, waits for them, and re-layouts  2.94 us (3%)
  matrix products  2.41 us (3%)
  other arithmetic  2.05 us (2%)
    all_to_all x1, waiting for transfers between devices, on_device(): lax.all_to_all(packed.reshape(banks, SLOTS, half_model), 'aa', 0, 0, tile...  22.1 us
    all_to_all x1, starting transfers between devices, on_device(): lax.all_to_all(packed.reshape(banks, SLOTS, half_model), 'aa', 0, 0, tile...  21.9 us
    pallas_call x1, Pallas kernels, project(): pl.pallas_call(functools.partial(project_kernel, kvw // size, size), grid...  12.2 us
    all_to_all x1, starting transfers between devices, on_device(): lax.all_to_all(raised.reshape(banks, SLOTS, half_query), 'aa', 0, 0, tile...  7.67 us
    ppermute x1, starting transfers between devices, on_device(): low = low + lax.ppermute(low, 'ba', swap)  7.4 us
    pallas_call x1, Pallas kernels, attend(): pl.pallas_call(functools.partial(attend_kernel, requests, tokens, heads,...  6.37 us
    all_to_all x1, waiting for transfers between devices, on_device(): lax.all_to_all(raised.reshape(banks, SLOTS, half_query), 'aa', 0, 0, tile...  3.71 us
    ppermute x1, starting transfers between devices, on_device(): got = lax.ppermute(sent, 'ba', swap)  2.94 us
  transfers between devices with their start and end apart: 4, of which 4 were waited for; matrix products, arithmetic and copies ran while one was open for 1% of the time, Pallas kernels for 13%

profile of v1, /device:TPU:513, one launch (start us, length us, event | category | flops | bytes accessed | tf_op | source)
XLA Modules:
  0.0 93.1 jit_solution(13797855812519110592)
XLA Ops:
  0.0 0.0 copy-start
  0.0 0.0 copy-start.2
  0.0 0.9 fusion.1
  0.9 0.7 fusion.12
  1.6 0.0 copy-done
  1.6 0.0 copy-start.3
  1.6 0.5 convolution_convert_fusion
  2.1 1.2 %reshape.51 = bf16[64,4,2048]{2,1,0:T(4,128)(2,1)} reshape(bf16[256,2048]{1,0:T(8,128)(2,1)S(1)} %convolution_convert_fusion) | data formatting | bytes 2097152 | tf_op jit(solution)/shard_map/reshape | solution.py:137
  3.3 0.0 copy-start.4
  3.3 21.9 %all-to-all-start = ((bf16[64,4,2048]{2,1,0:T(4,128)(2,1)}), bf16[64,4,2048]{2,1,0:T(4,128)(2,1)S(1)}, u32[]{:S(2)}, u32[]{:S(2)}) async-start(bf16[64,4,2048]{2,1,0:T(4,128)(2,1)} %reshape.51), calls=%async_computation | async-start | bytes 2097152 | tf_op jit(solution)/shard_map/all_to_all | solution.py:136
  25.3 22.1 %all-to-all-done = bf16[64,4,2048]{2,1,0:T(4,128)(2,1)S(1)} async-done(((bf16[64,4,2048]{2,1,0:T(4,128)(2,1)}), bf16[64,4,2048]{2,1,0:T(4,128)(2,1)S(1)}, u32[]{:S(2)}, u32[]{:S(2)}) %all-to-all-start) | async-done | bytes 1048608 | tf_op jit(solution)/shard_map/all_to_all | solution.py:136
  47.4 0.3 reshape.52
  47.7 0.0 copy-done.2
  47.7 0.4 fusion.2
  48.1 7.4 %collective-permute-start = (f32[256,16]{0,1:T(8,128)S(1)}, f32[256,16]{0,1:T(8,128)S(1)}, u32[]{:S(2)}, u32[]{:S(2)}) collective-permute-start(f32[256,16]{0,1:T(8,128)S(1)} %fusion.2), channel_id=1, source_target_pairs={{0,1},{1,0},{2,3},{3,2},{4,5},{5,4},{6,7},{7,6},{8,9},{9,8},{10,11... | collective-permute-start | bytes 49160 | tf_op jit(solution)/shard_map/ppermute | solution.py:152
  55.5 0.8 collective-permute-done
  56.3 0.0 copy-done.3
  56.3 0.3 convolution_convert_fusion.1
  56.6 1.0 %reshape.54 = bf16[64,4,1024]{2,1,0:T(4,128)(2,1)} reshape(bf16[256,1024]{1,0:T(8,128)(2,1)S(1)} %convolution_convert_fusion.1) | data formatting | bytes 1048576 | tf_op jit(solution)/shard_map/reshape | solution.py:157
  57.6 7.7 %all-to-all-start.1 = ((bf16[64,4,1024]{2,1,0:T(4,128)(2,1)}), bf16[64,4,1024]{2,1,0:T(4,128)(2,1)S(1)}, u32[]{:S(2)}, u32[]{:S(2)}) async-start(bf16[64,4,1024]{2,1,0:T(4,128)(2,1)} %reshape.54), calls=%async_computation.1 | async-start | bytes 1048576 | tf_op jit(solution)/shard_map/all_to_all | solution.py:156
  65.3 0.0 copy-done.4
  65.3 0.1 lt.41
  65.4 0.1 lt.43
  65.5 0.1 lt.38
  65.6 0.1 lt.39
  65.7 0.0 copy-start.1
  65.7 12.2 %project.1 = (bf16[768,512]{1,0:T(8,128)(2,1)}, bf16[768,512]{1,0:T(8,128)(2,1)}) custom-call(bf16[768,4096]{1,0:T(8,128)(2,1)} %bitcast.24, bf16[4096,512]{1,0:T(8,128)(2,1)} %wk_ref.1, bf16[4096,512]{1,0:T(8,128)(2,1)} %wv_ref.1, f32[1,128]{1,0:T(1,128)} %bitcast.26), custom_call_target="tpu_custom_call" | custom-call | flops 6442450944 | bytes 16252928 | tf_op jit(solution)/shard_map/project/pallas_call | solution.py:32
  77.8 3.7 %all-to-all-done.1 = bf16[64,4,1024]{2,1,0:T(4,128)(2,1)S(1)} async-done(((bf16[64,4,1024]{2,1,0:T(4,128)(2,1)}), bf16[64,4,1024]{2,1,0:T(4,128)(2,1)S(1)}, u32[]{:S(2)}, u32[]{:S(2)}) %all-to-all-start.1) | async-done | bytes 524320 | tf_op jit(solution)/shard_map/all_to_all | solution.py:156
  81.6 0.1 reshape.55
  81.7 0.0 copy-done.1
  81.7 0.3 fusion
  82.0 2.9 %collective-permute-start.1 = (bf16[64,1024]{1,0:T(8,128)(2,1)S(1)}, bf16[64,1024]{1,0:T(8,128)(2,1)S(1)}, u32[]{:S(2)}, u32[]{:S(2)}) collective-permute-start(bf16[64,1024]{1,0:T(8,128)(2,1)S(1)} %constant_dynamic-slice_fusion), channel_id=1, source_target_pairs={{0,1},{1,0},{2,3},{3,2},{4,5},{5,4},{6,7},{7,6},{8,9},{9,8},{10,11... | collective-permute-start | bytes 393224 | tf_op jit(solution)/shard_map/ppermute | solution.py:163
  84.9 0.6 compare_convert_fusion.valid_ref
  85.5 0.4 collective-permute-done.1
  85.9 0.1 broadcast_select_fusion.1
  86.0 0.7 pad_maximum_fusion.q_ref
  86.7 6.4 %attend.1 = bf16[64,2048]{1,0:T(8,128)(2,1)} custom-call(bf16[64,2048]{1,0:T(8,128)(2,1)} %pad_maximum_fusion.q_ref, bf16[12,64,512]{2,1,0:T(8,128)(2,1)} %bitcast.22, bf16[12,64,512]{2,1,0:T(8,128)(2,1)} %bitcast.23, f32[4,192]{1,0:T(4,128)} %compare_convert_fusion.valid_ref), custom_call_target="tpu_custom_call" | custom-call | flops 100663296 | bytes 2097152 | tf_op jit(solution)/shard_map/attend/pallas_call | solution.py:89
  (3 shorter events, 0.0 us)
Async XLA Ops:
  0.0 1.6 %copy-start = (bf16[128,2048]{1,0:T(8,128)(2,1)S(1)}, bf16[128,2048]{1,0:T(8,128)(2,1)}, u32[]{:S(2)}) copy-start(bf16[128,2048]{1,0:T(8,128)(2,1)} %param.14) | copy-start | bytes 1572868
  0.0 47.7 %copy-start.2 = (bf16[1,4096,16]{1,2,0:T(8,128)(2,1)S(1)}, bf16[1,4096,16]{1,2,0:T(8,128)(2,1)}, u32[]{:S(2)}) copy-start(bf16[1,4096,16]{1,2,0:T(8,128)(2,1)} %param.16) | copy-start | bytes 393220
  1.6 54.7 %copy-start.3 = (bf16[1,16,2048]{2,1,0:T(8,128)(2,1)S(1)}, bf16[1,16,2048]{2,1,0:T(8,128)(2,1)}, u32[]{:S(2)}) copy-start(bf16[1,16,2048]{2,1,0:T(8,128)(2,1)} %param.17) | copy-start | bytes 196612
  3.3 62.0 %copy-start.4 = (s32[64]{0:T(128)S(1)}, s32[64]{0:T(128)}, u32[]{:S(2)}) copy-start(s32[64]{0:T(128)} %param.19) | copy-start | bytes 772
  3.3 44.1 %all-to-all-start = ((bf16[64,4,2048]{2,1,0:T(4,128)(2,1)}), bf16[64,4,2048]{2,1,0:T(4,128)(2,1)S(1)}, u32[]{:S(2)}, u32[]{:S(2)}) async-start(bf16[64,4,2048]{2,1,0:T(4,128)(2,1)} %reshape.51), calls=%async_computation | async-start | bytes 2097152 | tf_op jit(solution)/shard_map/all_to_all | solution.py:136
  48.1 8.2 %collective-permute-start = (f32[256,16]{0,1:T(8,128)S(1)}, f32[256,16]{0,1:T(8,128)S(1)}, u32[]{:S(2)}, u32[]{:S(2)}) collective-permute-start(f32[256,16]{0,1:T(8,128)S(1)} %fusion.2), channel_id=1, source_target_pairs={{0,1},{1,0},{2,3},{3,2},{4,5},{5,4},{6,7},{7,6},{8,9},{9,8},{10,11... | collective-permute-start | bytes 49160 | tf_op jit(solution)/shard_map/ppermute | solution.py:152
  57.6 23.9 %all-to-all-start.1 = ((bf16[64,4,1024]{2,1,0:T(4,128)(2,1)}), bf16[64,4,1024]{2,1,0:T(4,128)(2,1)S(1)}, u32[]{:S(2)}, u32[]{:S(2)}) async-start(bf16[64,4,1024]{2,1,0:T(4,128)(2,1)} %reshape.54), calls=%async_computation.1 | async-start | bytes 1048576 | tf_op jit(solution)/shard_map/all_to_all | solution.py:156
  65.7 16.0 %copy-start.1 = (bf16[128,1024]{1,0:T(8,128)(2,1)S(1)}, bf16[128,1024]{1,0:T(8,128)(2,1)}, u32[]{:S(2)}) copy-start(bf16[128,1024]{1,0:T(8,128)(2,1)} %param.15) | copy-start | bytes 786436
  82.0 3.9 %collective-permute-start.1 = (bf16[64,1024]{1,0:T(8,128)(2,1)S(1)}, bf16[64,1024]{1,0:T(8,128)(2,1)S(1)}, u32[]{:S(2)}, u32[]{:S(2)}) collective-permute-start(bf16[64,1024]{1,0:T(8,128)(2,1)S(1)} %constant_dynamic-slice_fusion), channel_id=1, source_target_pairs={{0,1},{1,0},{2,3},{3,2},{4,5},{5,4},{6,7},{7,6},{8,9},{9,8},{10,11... | collective-permute-start | bytes 393224 | tf_op jit(solution)/shard_map/ppermute | solution.py:163

commit v2 on v1

v2 whole, which is shorter than its diff:
```python
import functools
import math

import jax
import jax.numpy as jnp
from jax import lax
from jax.experimental import pallas as pl
from jax.experimental.pallas import tpu as pltpu
from jax.sharding import PartitionSpec as P

TILE_TOKENS = 3
CHUNK = 16
SLOTS = 4
VMEM = pl.BlockSpec(memory_space=pltpu.VMEM)
SMEM = pl.BlockSpec(memory_space=pltpu.SMEM)


def call(kernel, ins, out, name, flops, limit=24):
    outs = jax.tree.leaves(out)
    specs = [SMEM if v.ndim == 1 else VMEM for v in ins]
    return pl.pallas_call(
        kernel,
        out_shape=out,
        in_specs=specs,
        out_specs=jax.tree.map(lambda _: VMEM, out),
        compiler_params=pltpu.CompilerParams(vmem_limit_bytes=limit * 2**20),
        cost_estimate=pl.CostEstimate(
            flops=flops,
            bytes_accessed=sum(v.size * v.dtype.itemsize for v in [*ins, *outs]),
            transcendentals=0,
        ),
        name=name,
    )(*ins)


def project_kernel(heads, size, x_ref, wk_ref, wv_ref, gain_ref, keys_ref, values_ref):
    x = x_ref[...]
    raw = jnp.dot(x, wk_ref[...], preferred_element_type=jnp.float32)
    for h in range(heads):
        part = raw[:, h * size : (h + 1) * size]
        scale = lax.rsqrt(jnp.mean(part * part, axis=-1, keepdims=True) + 1e-06)
        keys_ref[:, h * size : (h + 1) * size] = (part * scale * gain_ref[...]).astype(jnp.bfloat16)
    values_ref[...] = jnp.dot(x, wv_ref[...], preferred_element_type=jnp.float32).astype(jnp.bfloat16)


def project(x, wk, wv, gain):
    rows, width = x.shape
    kvw = wk.shape[1]
    size = gain.shape[1]
    tile = rows // 6 if rows % 96 == 0 else rows
    whole = lambda i: (0, 0)
    return pl.pallas_call(
        functools.partial(project_kernel, kvw // size, size),
        grid=(rows // tile,),
        in_specs=[
            pl.BlockSpec((tile, width), lambda i: (i, 0)),
            pl.BlockSpec((width, kvw), whole),
            pl.BlockSpec((width, kvw), whole),
            pl.BlockSpec((1, size), whole),
        ],
        out_specs=[pl.BlockSpec((tile, kvw), lambda i: (i, 0))] * 2,
        out_shape=[jax.ShapeDtypeStruct((rows, kvw), jnp.bfloat16)] * 2,
        compiler_params=pltpu.CompilerParams(vmem_limit_bytes=40 * 2**20),
        cost_estimate=pl.CostEstimate(
            flops=4 * rows * width * kvw,
            bytes_accessed=2 * (rows * width + 2 * width * kvw + 2 * rows * kvw),
            transcendentals=0,
        ),
        name="project",
    )(x, wk, wv, gain)


def pack_kernel(side, core_ref, owner_ref, mine_ref, other_ref, bank_ref, out_ref, slot_ref):
    requests = owner_ref.shape[1]
    held = side // 2 * SLOTS
    core = core_ref[0]
    names = owner_ref[...]
    across = jnp.broadcast_to(names.astype(jnp.float32), (requests, requests))
    down = jnp.transpose(across)
    low = lax.broadcasted_iota(jnp.int32, (requests, requests), 0)
    high = lax.broadcasted_iota(jnp.int32, (requests, requests), 1)
    earlier = jnp.where((across == down) & (low < high), 1.0, 0.0)
    rank = jnp.sum(earlier, axis=0, keepdims=True).astype(jnp.int32)
    column = names % side
    line = names // side
    peer = jnp.where(core == 0, column, line)
    which = jnp.where(core == 0, line, column) // 2
    slot = jnp.where((column + line) % 2 == core, peer * held + which * SLOTS + rank, -1)
    slot_ref[...] = jnp.broadcast_to(slot, slot_ref.shape)
    row = lax.broadcasted_iota(jnp.int32, (side * held, requests), 0)
    placing = jnp.where(row == slot, 1.0, 0.0).astype(jnp.bfloat16)
    mine = jnp.dot(placing, mine_ref[...], preferred_element_type=jnp.float32).astype(jnp.bfloat16)
    other = jnp.dot(placing, other_ref[...], preferred_element_type=jnp.float32).astype(
        jnp.bfloat16
    )
    for p in range(side):
        out_ref[p, :held] = mine[p * held : (p + 1) * held]
        out_ref[p, held : 2 * held] = other[p * held : (p + 1) * held]
        out_ref[p, 2 * held :] = bank_ref[...]


def raise_kernel(side, rank, rows_ref, bank_ref, out_ref):
    held = side // 2 * SLOTS
    half = rank // 2
    width = rows_ref.shape[2]
    mine = rows_ref[:, :held].reshape(side * held, width)
    other = rows_ref[:, held : 2 * held].reshape(side * held, width)
    first = bank_ref[:, :half].reshape(side * half, width)
    second = bank_ref[:, half : 2 * half].reshape(side * half, width)
    up = bank_ref[:, 2 * half :].reshape(side * half, width)
    contract = (((1,), (1,)), ((), ()))
    low = lax.dot_general(mine, first, contract, preferred_element_type=jnp.float32)
    low = low + lax.dot_general(other, second, contract, preferred_element_type=jnp.float32)
    row = lax.broadcasted_iota(jnp.int32, low.shape, 0)
    col = lax.broadcasted_iota(jnp.int32, low.shape, 1)
    low = jnp.where((row // SLOTS) % (side // 2) == col // rank, low, 0.0).astype(jnp.bfloat16)
    raised = jnp.dot(low, up, preferred_element_type=jnp.float32).astype(jnp.bfloat16)
    out_ref[...] = raised.reshape(side, held, width)


def unpack_kernel(core_ref, slot_ref, back_ref, mine_ref, other_ref, whole):
    requests = slot_ref.shape[1]
    here = mine_ref.shape[0]
    core = core_ref[0]
    slots = back_ref.shape[0]
    row = lax.broadcasted_iota(jnp.int32, (slots, requests), 0)
    placing = jnp.where(row == slot_ref[:1], 1.0, 0.0).astype(jnp.bfloat16)
    whole[...] = lax.dot_general(
        placing, back_ref[...], (((0,), (0,)), ((), ())), preferred_element_type=jnp.float32
    )
    mine_ref[...] = whole[pl.ds(pl.multiple_of(core * here, here), here)].astype(jnp.bfloat16)
    other_ref[...] = whole[pl.ds(pl.multiple_of((1 - core) * here, here), here)].astype(
        jnp.bfloat16
    )


def attend_kernel(
    tokens, heads, group, size, mine_ref, got_ref, base_ref, k_ref, v_ref, valid_ref, out_ref
):
    requests = base_ref.shape[0]
    wide = tokens * CHUNK
    row = lax.broadcasted_iota(jnp.int32, (group * CHUNK, wide), 0)
    col = lax.broadcasted_iota(jnp.int32, (group * CHUNK, wide), 1)
    same = (row % CHUNK) == (col % CHUNK)
    delta = mine_ref[...].astype(jnp.float32) + got_ref[...].astype(jnp.float32)
    query = (base_ref[...].astype(jnp.float32) + delta).astype(jnp.bfloat16)
    for c in range(requests // CHUNK):
        rows = slice(c * CHUNK, (c + 1) * CHUNK)
        use = same & (valid_ref[c : c + 1, :] > 0.0)
        scores = []
        for h in range(heads):
            q = jnp.concatenate(
                [
                    query[rows, (h * group + g) * size : (h * group + g + 1) * size]
                    for g in range(group)
                ],
                axis=0,
            )
            k = k_ref[:, rows, h * size : (h + 1) * size].reshape(wide, size)
            scores.append(
                lax.dot_general(q, k, (((1,), (1,)), ((), ())), preferred_element_type=jnp.float32)
                / math.sqrt(size)
            )
        done = []
        for h in range(heads):
            masked = jnp.where(use, scores[h], -jnp.inf)
            weights = jnp.exp(masked - jnp.max(masked, axis=-1, keepdims=True))
            total = jnp.sum(weights, axis=-1, keepdims=True)
            v = v_ref[:, rows, h * size : (h + 1) * size].reshape(wide, size)
            weighted = jnp.dot(weights.astype(jnp.bfloat16), v, preferred_element_type=jnp.float32)
            done.append((weighted / total).astype(jnp.bfloat16))
        for h in range(heads):
            for g in range(group):
                out_ref[rows, (h * group + g) * size : (h * group + g + 1) * size] = done[h][
                    g * CHUNK : (g + 1) * CHUNK
                ]


def on_device(
    images,
    key_projection,
    value_projection,
    key_norm_gain,
    hidden,
    shared_query_base,
    adapter_down_matrix,
    adapter_up_matrix,
    tenant_adapter_index,
    used_tile_count,
):
    requests, half_model = hidden.shape
    half_query = shared_query_base.shape[1]
    size = key_norm_gain.shape[0]
    rank, width_query = adapter_up_matrix.shape[1:]
    here, tokens, width = images.shape
    banks = lax.axis_size("aa")
    side = math.isqrt(banks)
    assert side * side == banks and width_query == half_model
    held = side // 2 * SLOTS
    half = rank // 2
    both = ("aa", "ba")
    spot = range(side)
    lines = [[2 * (y * side + x) for x in spot] for y in spot]
    lines += [[2 * (y * side + x) + 1 for y in spot] for x in spot]
    beside = [(line[i], line[i ^ 1]) for line in lines for i in spot]
    swap = [(0, 1), (1, 0)]
    core = lax.axis_index("ba")
    bank = lax.axis_index("aa")
    column, line = bank % side, bank // side
    position = jnp.where(core == 0, column, line)
    flag = core.astype(jnp.int32).reshape(1)

    far_hidden = lax.ppermute(hidden, "ba", swap)

    halves = adapter_down_matrix[0].T.reshape(2, half, 2, half_model)
    whole = jnp.concatenate(
        [
            jnp.where(core == 0, halves[:, :, 1], halves[:, :, 0]),
            jnp.where(core == 0, halves[:, :, 0], halves[:, :, 1]),
            adapter_up_matrix[0].reshape(2, half, width_query),
        ],
        axis=1,
    )
    odd = position % 2 == 1
    ours = jnp.where(odd, whole[1], whole[0])
    theirs = lax.ppermute(jnp.where(odd, whole[0], whole[1]), both, beside)
    sent_bank = jnp.where((column + line) % 2 == 1 - core, ours, theirs)

    packed, slot = call(
        functools.partial(pack_kernel, side),
        [flag, tenant_adapter_index.reshape(1, requests), hidden, far_hidden, sent_bank],
        [
            jax.ShapeDtypeStruct((side, 2 * held + 3 * half, half_model), jnp.bfloat16),
            jax.ShapeDtypeStruct((8, requests), jnp.int32),
        ],
        "pack",
        4 * side * held * requests * half_model,
    )
    received = lax.all_to_all(packed, both, 0, 0, axis_index_groups=lines, tiled=True)

    x = images.transpose(1, 0, 2).reshape(tokens * here, width)
    keys, values = project(x, key_projection, value_projection, key_norm_gain[None, :])
    kept = lax.dynamic_slice_in_dim(shared_query_base, core * here, here, 0)
    sent = lax.dynamic_slice_in_dim(shared_query_base, (1 - core) * here, here, 0)
    got = lax.ppermute(sent, "ba", swap)
    base = jnp.concatenate(
        [jnp.where(core == 0, kept, got), jnp.where(core == 0, got, kept)], axis=1
    )
    tile = jnp.arange(tokens, dtype=jnp.int32) // TILE_TOKENS
    valid = tile[None, :, None] < used_tile_count.reshape(here // CHUNK, 1, CHUNK)
    valid = valid.astype(jnp.float32).reshape(here // CHUNK, tokens * CHUNK)
    received, keys, values, base, valid = lax.optimization_barrier(
        (received, keys, values, base, valid)
    )

    bank_rows = lax.ppermute(received[:, 2 * held :], "ba", swap)
    raised = call(
        functools.partial(raise_kernel, side, rank),
        [received, bank_rows],
        jax.ShapeDtypeStruct((side, held, width_query), jnp.bfloat16),
        "raise",
        6 * side * held * side * half * half_model,
    )
    back = lax.all_to_all(raised, both, 0, 0, axis_index_groups=lines, tiled=True)
    back = back.reshape(side * held, width_query)
    part = jax.ShapeDtypeStruct((here, width_query), jnp.bfloat16)
    mine, other = pl.pallas_call(
        unpack_kernel,
        out_shape=[part, part],
        in_specs=[SMEM, VMEM, VMEM],
        out_specs=[VMEM, VMEM],
        scratch_shapes=[pltpu.VMEM((requests, width_query), jnp.float32)],
        compiler_params=pltpu.CompilerParams(vmem_limit_bytes=24 * 2**20),
        cost_estimate=pl.CostEstimate(
            flops=2 * side * held * requests * width_query,
            bytes_accessed=4 * back.size,
            transcendentals=0,
        ),
        name="unpack",
    )(flag, slot, back)
    rest = lax.ppermute(other, "ba", swap)
    kvw = key_projection.shape[1]
    return call(
        functools.partial(attend_kernel, tokens, kvw // size, width_query // kvw, size),
        [
            mine,
            rest,
            base,
            keys.reshape(tokens, here, kvw),
            values.reshape(tokens, here, kvw),
            valid,
        ],
        jax.ShapeDtypeStruct((here, width_query), jnp.bfloat16),
        "attend",
        4 * here * width_query * tokens * CHUNK,
    )


def solution(mesh):
    placed = (
        P(("ga", "aa", "ba"), None, None),
        P(),
        P(),
        P(),
        P(("ga", "aa"), "ba"),
        P(("ga", "aa"), "ba"),
        P("aa", None, None),
        P("aa", None, None),
        P(("ga", "aa"), None),
        P(("ga", "aa", "ba")),
    )
    return jax.shard_map(
        on_device,
        mesh=mesh,
        in_specs=placed,
        out_specs=P(("ga", "aa", "ba"), None),
        check_vma=False,
    )
```

time: 93.5 us -> 85.4 us (0.913)
  waiting for transfers between devices: 27.1 us -> 11.2 us
  blocking collectives: 0 us -> 14.6 us
  local copies, waits for them, and re-layouts: 2.94 us -> 9.84 us
  Pallas kernels: 18.5 us -> 12.8 us
  starting transfers between devices: 39.9 us -> 35.2 us
  matrix products: 2.41 us -> 0 us
  other arithmetic: 2.05 us -> 1.06 us
    all_to_all x2 -> x1, starting transfers between devices: 29.6 us -> 3.8 us  [on_device(): lax.all_to_all(packed, both, 0, 0, axis_index_groups=lines, tiled=True)]
    ppermute x1 -> x4, starting transfers between devices: 7.4 us -> 28.5 us  [the longest x1 17.2 us: on_device(): far_hidden = lax.ppermute(hidden, 'ba', swap)]
    all_to_all x2 -> x1, waiting for transfers between devices: 25.9 us -> 6.39 us  [on_device(): lax.all_to_all(packed, both, 0, 0, axis_index_groups=lines, tiled=True)]
    all_to_all x0 -> x1, blocking collectives: none -> 14.6 us  [on_device(): lax.all_to_all(raised, both, 0, 0, axis_index_groups=lines, tiled=True)]
    unnamed x10 -> x20, local copies, waits for them, and re-layouts: 0.02 us -> 8.23 us
    ppermute x1 -> x4, waiting for transfers between devices: 0.84 us -> 4.8 us  [the longest x1 1.91 us: on_device(): bank_rows = lax.ppermute(received[:, 2 * held:], 'ba', swap)]
    pallas_call x1, Pallas kernels: 12.2 us -> 8.83 us  [project(): pl.pallas_call(functools.partial(project_kernel, kvw // size, size), grid...]
    dot_general x5 -> x0, matrix products: 2.41 us -> none  [the longest x1 0.9 us: on_device(): jnp.dot(lower.astype(jnp.bfloat16), hot.astype(jnp.bfloat16), preferred_e...]
  transfers between devices with their start and end apart: 4 -> 6, of which waited for: 4 -> 4; matrix products, arithmetic and copies ran while one was open for 1% -> 1% of each run, Pallas kernels for 13% -> 10%
where the time goes in v2:
time: 85.4 us; the launch traced here: 84.9 us
  starting transfers between devices  35.2 us (41%)
  blocking collectives  14.6 us (17%)
  Pallas kernels  12.8 us (15%)
  waiting for transfers between devices  11.2 us (13%)
  local copies, waits for them, and re-layouts  9.84 us (12%)
  other arithmetic  1.06 us (1%)
    ppermute x1, starting transfers between devices, on_device(): far_hidden = lax.ppermute(hidden, 'ba', swap)  17.2 us
    all_to_all x1, blocking collectives, on_device(): lax.all_to_all(raised, both, 0, 0, axis_index_groups=lines, tiled=True)  14.6 us
    pallas_call x1, Pallas kernels, project(): pl.pallas_call(functools.partial(project_kernel, kvw // size, size), grid...  8.83 us
    unnamed x20, local copies, waits for them, and re-layouts  8.23 us
    all_to_all x1, waiting for transfers between devices, on_device(): lax.all_to_all(packed, both, 0, 0, axis_index_groups=lines, tiled=True)  6.39 us
    ppermute x1, starting transfers between devices, on_device(): bank_rows = lax.ppermute(received[:, 2 * held:], 'ba', swap)  6.24 us
    all_to_all x1, starting transfers between devices, on_device(): lax.all_to_all(packed, both, 0, 0, axis_index_groups=lines, tiled=True)  3.8 us
    pallas_call x3, Pallas kernels, call(): pl.pallas_call(kernel, out_shape=out, in_specs=specs, out_specs=jax.tree....  3.61 us
  transfers between devices with their start and end apart: 6, of which 4 were waited for; matrix products, arithmetic and copies ran while one was open for 1% of the time, Pallas kernels for 10%

profile of v2, /device:TPU:513, one launch (start us, length us, event | category | flops | bytes accessed | tf_op | source)
XLA Modules:
  0.0 84.9 jit_solution(7426110823283438741)
XLA Ops:
  0.0 0.0 copy-start.8
  0.0 0.0 copy-start.9
  0.0 0.0 copy-start.7
  0.1 1.0 %reshape.49 = bf16[2,8,2,2048]{3,2,1,0:T(2,128)(2,1)S(1)} reshape(bf16[16,4096]{1,0:T(8,128)(2,1)} %bitcast.26) | data formatting | bytes 262144 | tf_op jit(solution)/shard_map/reshape | solution.py:215
  1.1 0.2 fusion
  1.3 0.1 select_bitcast_fusion.2
  1.4 0.9 %pad_maximum_fusion.1 = bf16[2,24,2048]{2,1,0:T(8,128)(2,1)S(1)} fusion(bf16[2,8,2048]{2,1,0:T(8,128)(2,1)} %bitcast.27, bf16[2,8,2048]{2,1,0:T(8,128)(2,1)S(1)} %get-tuple-element.30, bf16[2,8,2048]{2,1,0:T(8,128)(2,1)S(1)} %get-tuple-element.29), kind=kLoop, calls=%fused_computation.1 | loop fusion | flops 589824 | bytes 393216 | tf_op jit(solution)/shard_map/concatenate | solution.py:216
  2.3 3.4 %collective-permute-start.1 = (bf16[24,2048]{1,0:T(8,128)(2,1)S(1)}, bf16[24,2048]{1,0:T(8,128)(2,1)S(1)}, u32[]{:S(2)}, u32[]{:S(2)}) collective-permute-start(bf16[24,2048]{1,0:T(8,128)(2,1)S(1)} %select_bitcast_fusion), channel_id=1, source_target_pairs={{0,2},{2,0},{4,6},{6,4},{8,10},{10,8},{12,14},{14,12},{16,18},{18,... | collective-permute-start | bytes 294920 | tf_op jit(solution)/shard_map/ppermute | solution.py:226
  5.7 17.2 %collective-permute-start = (bf16[128,2048]{1,0:T(8,128)(2,1)}, bf16[128,2048]{1,0:T(8,128)(2,1)S(1)}, u32[]{:S(2)}, u32[]{:S(2)}) collective-permute-start(bf16[128,2048]{1,0:T(8,128)(2,1)} %mine_ref.1), channel_id=1, source_target_pairs={{0,1},{1,0},{2,3},{3,2},{4,5},{5,4},{6,7},{7,6},{8,9},{9,8},{10,11... | collective-permute-start | bytes 1572872 | tf_op jit(solution)/shard_map/ppermute | solution.py:213
  22.9 0.0 collective-permute-done.1
  22.9 1.7 %collective-permute-done.other_ref = bf16[128,2048]{1,0:T(8,128)(2,1)S(1)} collective-permute-done((bf16[128,2048]{1,0:T(8,128)(2,1)}, bf16[128,2048]{1,0:T(8,128)(2,1)S(1)}, u32[]{:S(2)}, u32[]{:S(2)}) %collective-permute-start) | collective-permute-done | bytes 524320 | tf_op jit(solution)/shard_map/ppermute | solution.py:213
  24.6 0.0 copy-start.3
  24.6 1.0 %copy-done.3 = bf16[128,2048]{1,0:T(8,128)(2,1)S(1)} copy-done((bf16[128,2048]{1,0:T(8,128)(2,1)S(1)}, bf16[128,2048]{1,0:T(8,128)(2,1)}, u32[]{:S(2)}) %copy-start.3) | copy-done | bytes 524312
  25.7 0.0 copy-start.4
  25.7 0.7 copy-done.4
  26.3 0.5 pack.1
  26.8 0.0 copy-start
  26.9 1.3 %copy-done = bf16[8,56,2048]{2,1,0:T(8,128)(2,1)} copy-done((bf16[8,56,2048]{2,1,0:T(8,128)(2,1)}, bf16[8,56,2048]{2,1,0:T(8,128)(2,1)S(1)}, u32[]{:S(2)}) %copy-start) | copy-done | bytes 1835032
  28.1 3.8 %all-to-all-start = ((bf16[8,56,2048]{2,1,0:T(8,128)(2,1)}), bf16[8,56,2048]{2,1,0:T(8,128)(2,1)S(1)}, u32[]{:S(2)}, u32[]{:S(2)}) async-start(bf16[8,56,2048]{2,1,0:T(8,128)(2,1)} %copy-done), calls=%async_computation | async-start | bytes 3670016 | tf_op jit(solution)/shard_map/all_to_all | solution.py:239
  31.9 0.0 copy-done.8
  32.0 2.9 %collective-permute-start.2 = (bf16[64,1024]{1,0:T(8,128)(2,1)S(1)}, bf16[64,1024]{1,0:T(8,128)(2,1)S(1)}, u32[]{:S(2)}, u32[]{:S(2)}) collective-permute-start(bf16[64,1024]{1,0:T(8,128)(2,1)S(1)} %constant_dynamic-slice_fusion), channel_id=1, source_target_pairs={{0,1},{1,0},{2,3},{3,2},{4,5},{5,4},{6,7},{7,6},{8,9},{9,8},{10,11... | collective-permute-start | bytes 393224 | tf_op jit(solution)/shard_map/ppermute | solution.py:245
  34.8 0.0 copy-done.9
  34.8 0.1 lt.50
  34.9 0.1 lt.47
  35.0 0.1 lt.48
  35.1 0.1 lt.52
  35.2 0.0 copy-done.7
  35.2 0.0 copy-start.5
  35.2 2.2 %copy-done.5 = bf16[4096,512]{1,0:T(8,128)(2,1)S(1)} copy-done((bf16[4096,512]{1,0:T(8,128)(2,1)S(1)}, bf16[4096,512]{1,0:T(8,128)(2,1)}, u32[]{:S(2)}) %copy-start.5) | copy-done | bytes 4194328
  37.4 0.0 copy-start.6
  37.4 2.2 %copy-done.6 = bf16[4096,512]{1,0:T(8,128)(2,1)S(1)} copy-done((bf16[4096,512]{1,0:T(8,128)(2,1)S(1)}, bf16[4096,512]{1,0:T(8,128)(2,1)}, u32[]{:S(2)}) %copy-start.6) | copy-done | bytes 4194328
  39.6 8.8 %project.1 = (bf16[768,512]{1,0:T(8,128)(2,1)S(1)}, bf16[768,512]{1,0:T(8,128)(2,1)S(1)}) custom-call(bf16[768,4096]{1,0:T(8,128)(2,1)} %bitcast.28, bf16[4096,512]{1,0:T(8,128)(2,1)S(1)} %copy-done.5, bf16[4096,512]{1,0:T(8,128)(2,1)S(1)} %copy-done.6, f32[1,128]{1,0:T(1,128)S(1)} %bitcast.25), custom_call_target="tpu_custom_call" | custom-call | flops 6442450944 | bytes 16252928 | tf_op jit(solution)/shard_map/project/pallas_call | solution.py:52
  48.4 0.0 copy-start.1
  48.4 0.9 %copy-done.1 = bf16[768,512]{1,0:T(8,128)(2,1)} copy-done((bf16[768,512]{1,0:T(8,128)(2,1)}, bf16[768,512]{1,0:T(8,128)(2,1)S(1)}, u32[]{:S(2)}) %copy-start.1) | copy-done | bytes 786456
  49.3 0.0 collective-permute-done.2
  49.3 0.1 broadcast_select_fusion.1
  49.4 6.4 %all-to-all-done.rows_ref = bf16[8,56,2048]{2,1,0:T(8,128)(2,1)S(1)} async-done(((bf16[8,56,2048]{2,1,0:T(8,128)(2,1)}), bf16[8,56,2048]{2,1,0:T(8,128)(2,1)S(1)}, u32[]{:S(2)}, u32[]{:S(2)}) %all-to-all-start) | async-done | bytes 1835040 | tf_op jit(solution)/shard_map/all_to_all | solution.py:239
  55.8 0.0 copy-start.2
  55.8 0.1 slice.23
  55.8 6.2 %collective-permute-start.3 = (bf16[8,24,2048]{2,1,0:T(8,128)(2,1)S(1)}, bf16[8,24,2048]{2,1,0:T(8,128)(2,1)S(1)}, u32[]{:S(2)}, u32[]{:S(2)}) collective-permute-start(bf16[8,24,2048]{2,1,0:T(8,128)(2,1)S(1)} %slice.23), channel_id=1, source_target_pairs={{0,1},{1,0},{2,3},{3,2},{4,5},{5,4},{6,7},{7,6},{8,9},{9,8},{10,11... | collective-permute-start | bytes 2359304 | tf_op jit(solution)/shard_map/ppermute | solution.py:256
  62.1 1.9 %collective-permute-done.3.bank_ref = bf16[8,24,2048]{2,1,0:T(8,128)(2,1)S(1)} collective-permute-done((bf16[8,24,2048]{2,1,0:T(8,128)(2,1)S(1)}, bf16[8,24,2048]{2,1,0:T(8,128)(2,1)S(1)}, u32[]{:S(2)}, u32[]{:S(2)}) %collective-permute-start.3) | collective-permute-done | bytes 786464 | tf_op jit(solution)/shard_map/ppermute | solution.py:256
  64.0 0.9 %raise.1 = bf16[8,16,2048]{2,1,0:T(8,128)(2,1)S(1)} custom-call(bf16[8,56,2048]{2,1,0:T(8,128)(2,1)S(1)} %all-to-all-done.rows_ref, bf16[8,24,2048]{2,1,0:T(8,128)(2,1)S(1)} %collective-permute-done.3.bank_ref), custom_call_target="tpu_custom_call" | custom-call | flops 100663296 | bytes 3145728 | tf_op jit(solution)/shard_map/raise/pallas_call | solution.py:21
  64.9 14.6 %all_to_all.10 = bf16[8,16,2048]{2,1,0:T(8,128)(2,1)S(1)} all-to-all(bf16[8,16,2048]{2,1,0:T(8,128)(2,1)S(1)} %raise.1), channel_id=1, replica_groups={{0,2,4,6,8,10,12,14},{16,18,20,22,24,26,28,30},{32,34,36,38,40,42,44,46..., dimensions={0} | all-to-all | bytes 1048576 | tf_op jit(solution)/shard_map/all_to_all | solution.py:264
  79.5 0.4 unpack.1
  79.9 1.6 %collective-permute-start.4 = (bf16[64,2048]{1,0:T(8,128)(2,1)S(1)}, bf16[64,2048]{1,0:T(8,128)(2,1)S(1)}, u32[]{:S(2)}, u32[]{:S(2)}) collective-permute-start(bf16[64,2048]{1,0:T(8,128)(2,1)S(1)} %get-tuple-element.22), channel_id=1, source_target_pairs={{0,1},{1,0},{2,3},{3,2},{4,5},{5,4},{6,7},{7,6},{8,9},{9,8},{10,11... | collective-permute-start | bytes 786440 | tf_op jit(solution)/shard_map/ppermute | solution.py:281
  81.5 1.2 %collective-permute-done.4.got_ref = bf16[64,2048]{1,0:T(8,128)(2,1)S(1)} collective-permute-done((bf16[64,2048]{1,0:T(8,128)(2,1)S(1)}, bf16[64,2048]{1,0:T(8,128)(2,1)S(1)}, u32[]{:S(2)}, u32[]{:S(2)}) %collective-permute-start.4) | collective-permute-done | bytes 262176 | tf_op jit(solution)/shard_map/ppermute | solution.py:281
  82.7 0.0 copy-done.2
  82.7 2.2 %attend.1 = bf16[64,2048]{1,0:T(8,128)(2,1)} custom-call(bf16[64,2048]{1,0:T(8,128)(2,1)S(1)} %get-tuple-element.21.mine_ref, bf16[64,2048]{1,0:T(8,128)(2,1)S(1)} %collective-permute-done.4.got_ref, bf16[64,2048]{1,0:T(8,128)(2,1)S(1)} %pad_maximum_fusion.base_ref, bf16[12,64,512]{2,1,0:T(8,128)(2,1)S(1)} %bitcast.22, bf16[12,64,512]{2,1,0:T(8,128)(2,1)S(1)} %bitcast.23, ...), custom_call_target="tpu_custom_call" | custom-call | flops 100663296 | bytes 2624512 | tf_op jit(solution)/shard_map/attend/pallas_call | solution.py:21
  (7 shorter events, 0.1 us)
Async XLA Ops:
  0.0 31.9 %copy-start.8 = (bf16[128,1024]{1,0:T(8,128)(2,1)S(1)}, bf16[128,1024]{1,0:T(8,128)(2,1)}, u32[]{:S(2)}) copy-start(bf16[128,1024]{1,0:T(8,128)(2,1)} %param.15) | copy-start | bytes 786436
  0.0 34.8 %copy-start.9 = (s32[64]{0:T(128)S(1)}, s32[64]{0:T(128)}, u32[]{:S(2)}) copy-start(s32[64]{0:T(128)} %param.19) | copy-start | bytes 772
  0.0 35.2 %copy-start.7 = (f32[128]{0:T(128)S(1)}, f32[128]{0:T(128)}, u32[]{:S(2)}) copy-start(f32[128]{0:T(128)} %param.13) | copy-start | bytes 1540
  2.3 20.6 %collective-permute-start.1 = (bf16[24,2048]{1,0:T(8,128)(2,1)S(1)}, bf16[24,2048]{1,0:T(8,128)(2,1)S(1)}, u32[]{:S(2)}, u32[]{:S(2)}) collective-permute-start(bf16[24,2048]{1,0:T(8,128)(2,1)S(1)} %select_bitcast_fusion), channel_id=1, source_target_pairs={{0,2},{2,0},{4,6},{6,4},{8,10},{10,8},{12,14},{14,12},{16,18},{18,... | collective-permute-start | bytes 294920 | tf_op jit(solution)/shard_map/ppermute | solution.py:226
  5.7 18.9 %collective-permute-start = (bf16[128,2048]{1,0:T(8,128)(2,1)}, bf16[128,2048]{1,0:T(8,128)(2,1)S(1)}, u32[]{:S(2)}, u32[]{:S(2)}) collective-permute-start(bf16[128,2048]{1,0:T(8,128)(2,1)} %mine_ref.1), channel_id=1, source_target_pairs={{0,1},{1,0},{2,3},{3,2},{4,5},{5,4},{6,7},{7,6},{8,9},{9,8},{10,11... | collective-permute-start | bytes 1572872 | tf_op jit(solution)/shard_map/ppermute | solution.py:213
  24.6 1.0 %copy-start.3 = (bf16[128,2048]{1,0:T(8,128)(2,1)S(1)}, bf16[128,2048]{1,0:T(8,128)(2,1)}, u32[]{:S(2)}) copy-start(bf16[128,2048]{1,0:T(8,128)(2,1)} %mine_ref.1) | copy-start | bytes 1572868
  25.7 0.7 copy-start.4
  26.8 1.3 %copy-start = (bf16[8,56,2048]{2,1,0:T(8,128)(2,1)}, bf16[8,56,2048]{2,1,0:T(8,128)(2,1)S(1)}, u32[]{:S(2)}) copy-start(bf16[8,56,2048]{2,1,0:T(8,128)(2,1)S(1)} %get-tuple-element.17) | copy-start | bytes 5505028
  28.1 27.7 %all-to-all-start = ((bf16[8,56,2048]{2,1,0:T(8,128)(2,1)}), bf16[8,56,2048]{2,1,0:T(8,128)(2,1)S(1)}, u32[]{:S(2)}, u32[]{:S(2)}) async-start(bf16[8,56,2048]{2,1,0:T(8,128)(2,1)} %copy-done), calls=%async_computation | async-start | bytes 3670016 | tf_op jit(solution)/shard_map/all_to_all | solution.py:239
  32.0 17.3 %collective-permute-start.2 = (bf16[64,1024]{1,0:T(8,128)(2,1)S(1)}, bf16[64,1024]{1,0:T(8,128)(2,1)S(1)}, u32[]{:S(2)}, u32[]{:S(2)}) collective-permute-start(bf16[64,1024]{1,0:T(8,128)(2,1)S(1)} %constant_dynamic-slice_fusion), channel_id=1, source_target_pairs={{0,1},{1,0},{2,3},{3,2},{4,5},{5,4},{6,7},{7,6},{8,9},{9,8},{10,11... | collective-permute-start | bytes 393224 | tf_op jit(solution)/shard_map/ppermute | solution.py:245
  35.2 2.2 %copy-start.5 = (bf16[4096,512]{1,0:T(8,128)(2,1)S(1)}, bf16[4096,512]{1,0:T(8,128)(2,1)}, u32[]{:S(2)}) copy-start(bf16[4096,512]{1,0:T(8,128)(2,1)} %wk_ref.1) | copy-start | bytes 12582916
  37.4 2.2 %copy-start.6 = (bf16[4096,512]{1,0:T(8,128)(2,1)S(1)}, bf16[4096,512]{1,0:T(8,128)(2,1)}, u32[]{:S(2)}) copy-start(bf16[4096,512]{1,0:T(8,128)(2,1)} %wv_ref.1) | copy-start | bytes 12582916
  48.4 0.9 %copy-start.1 = (bf16[768,512]{1,0:T(8,128)(2,1)}, bf16[768,512]{1,0:T(8,128)(2,1)S(1)}, u32[]{:S(2)}) copy-start(bf16[768,512]{1,0:T(8,128)(2,1)S(1)} %get-tuple-element.25) | copy-start | bytes 2359300
  55.8 26.9 %copy-start.2 = (bf16[768,512]{1,0:T(8,128)(2,1)S(1)}, bf16[768,512]{1,0:T(8,128)(2,1)}, u32[]{:S(2)}) copy-start(bf16[768,512]{1,0:T(8,128)(2,1)} %copy-done.1) | copy-start | bytes 2359300
  55.8 8.1 %collective-permute-start.3 = (bf16[8,24,2048]{2,1,0:T(8,128)(2,1)S(1)}, bf16[8,24,2048]{2,1,0:T(8,128)(2,1)S(1)}, u32[]{:S(2)}, u32[]{:S(2)}) collective-permute-start(bf16[8,24,2048]{2,1,0:T(8,128)(2,1)S(1)} %slice.23), channel_id=1, source_target_pairs={{0,1},{1,0},{2,3},{3,2},{4,5},{5,4},{6,7},{7,6},{8,9},{9,8},{10,11... | collective-permute-start | bytes 2359304 | tf_op jit(solution)/shard_map/ppermute | solution.py:256
  79.9 2.8 %collective-permute-start.4 = (bf16[64,2048]{1,0:T(8,128)(2,1)S(1)}, bf16[64,2048]{1,0:T(8,128)(2,1)S(1)}, u32[]{:S(2)}, u32[]{:S(2)}) collective-permute-start(bf16[64,2048]{1,0:T(8,128)(2,1)S(1)} %get-tuple-element.22), channel_id=1, source_target_pairs={{0,1},{1,0},{2,3},{3,2},{4,5},{5,4},{6,7},{7,6},{8,9},{9,8},{10,11... | collective-permute-start | bytes 786440 | tf_op jit(solution)/shard_map/ppermute | solution.py:281

commit v3 on v2

--- a/solution.py
+++ b/solution.py
@@ -15,7 +15,7 @@
 SMEM = pl.BlockSpec(memory_space=pltpu.SMEM)
 
 
-def call(kernel, ins, out, name, flops, limit=24):
+def call(kernel, ins, out, flops, limit=24):
     outs = jax.tree.leaves(out)
     specs = [SMEM if v.ndim == 1 else VMEM for v in ins]
     return pl.pallas_call(
@@ -29,7 +29,6 @@
             bytes_accessed=sum(v.size * v.dtype.itemsize for v in [*ins, *outs]),
             transcendentals=0,
         ),
-        name=name,
     )(*ins)
 
 
@@ -70,11 +69,46 @@
     )(x, wk, wv, gain)
 
 
-def pack_kernel(side, core_ref, owner_ref, mine_ref, other_ref, bank_ref, out_ref, slot_ref):
-    requests = owner_ref.shape[1]
+def cut_kernel(half, at_ref, down_ref, up_ref, ours_ref, theirs_ref):
+    core, odd = at_ref[0], at_ref[1]
+    width = ours_ref.shape[1]
+
+    def cut(out, low):
+        rows = slice(low * half, (low + 1) * half)
+
+        @pl.when(core == 0)
+        def _():
+            out[:half] = down_ref[rows, width:]
+            out[half : 2 * half] = down_ref[rows, :width]
+
+        @pl.when(core != 0)
+        def _():
+            out[:half] = down_ref[rows, :width]
+            out[half : 2 * half] = down_ref[rows, width:]
+
+        out[2 * half :] = up_ref[rows]
+
+    @pl.when(odd == 0)
+    def _():
+        cut(ours_ref, 0)
+        cut(theirs_ref, 1)
+
+    @pl.when(odd != 0)
+    def _():
+        cut(ours_ref, 1)
+        cut(theirs_ref, 0)
+
+
+def placing_of(slot, slots):
+    row = lax.broadcasted_iota(jnp.int32, (slots, slot.shape[1]), 0)
+    return jnp.where(row == slot, 1.0, 0.0).astype(jnp.bfloat16)
+
+
+def near_kernel(side, at_ref, names_ref, mine_ref, near_ref, slot_ref):
+    requests = names_ref.shape[1]
     held = side // 2 * SLOTS
-    core = core_ref[0]
-    names = owner_ref[...]
+    core = at_ref[0]
+    names = names_ref[...]
     across = jnp.broadcast_to(names.astype(jnp.float32), (requests, requests))
     down = jnp.transpose(across)
     low = lax.broadcasted_iota(jnp.int32, (requests, requests), 0)
@@ -83,20 +117,27 @@
     rank = jnp.sum(earlier, axis=0, keepdims=True).astype(jnp.int32)
     column = names % side
     line = names // side
-    peer = jnp.where(core == 0, column, line)
-    which = jnp.where(core == 0, line, column) // 2
-    slot = jnp.where((column + line) % 2 == core, peer * held + which * SLOTS + rank, -1)
+    peer = jnp.where(core == 0, line, column)
+    which = jnp.where(core == 0, column, line) // 2
+    slot = jnp.where((column + line) % 2 == 1 - core, peer * held + which * SLOTS + rank, -1)
     slot_ref[...] = jnp.broadcast_to(slot, slot_ref.shape)
-    row = lax.broadcasted_iota(jnp.int32, (side * held, requests), 0)
-    placing = jnp.where(row == slot, 1.0, 0.0).astype(jnp.bfloat16)
-    mine = jnp.dot(placing, mine_ref[...], preferred_element_type=jnp.float32).astype(jnp.bfloat16)
+    placing = placing_of(slot, side * held)
+    near_ref[...] = jnp.dot(placing, mine_ref[...], preferred_element_type=jnp.float32).astype(
+        jnp.bfloat16
+    )
+
+
+def far_kernel(side, at_ref, slot_ref, near_ref, other_ref, ours_ref, theirs_ref, out_ref):
+    held = side // 2 * SLOTS
+    placing = placing_of(slot_ref[:1], side * held)
     other = jnp.dot(placing, other_ref[...], preferred_element_type=jnp.float32).astype(
         jnp.bfloat16
     )
+    bank = jnp.where(at_ref[2] == at_ref[0], ours_ref[...], theirs_ref[...])
     for p in range(side):
-        out_ref[p, :held] = mine[p * held : (p + 1) * held]
+        out_ref[p, :held] = near_ref[p * held : (p + 1) * held]
         out_ref[p, held : 2 * held] = other[p * held : (p + 1) * held]
-        out_ref[p, 2 * held :] = bank_ref[...]
+        out_ref[p, 2 * held :] = bank
 
 
 def raise_kernel(side, rank, rows_ref, bank_ref, out_ref):
@@ -189,7 +230,6 @@
     used_tile_count,
 ):
     requests, half_model = hidden.shape
-    half_query = shared_query_base.shape[1]
     size = key_norm_gain.shape[0]
     rank, width_query = adapter_up_matrix.shape[1:]
     here, tokens, width = images.shape
@@ -200,41 +240,45 @@
     half = rank // 2
     both = ("aa", "ba")
     spot = range(side)
-    lines = [[2 * (y * side + x) for x in spot] for y in spot]
-    lines += [[2 * (y * side + x) + 1 for y in spot] for x in spot]
-    beside = [(line[i], line[i ^ 1]) for line in lines for i in spot]
+    lines = [[2 * (y * side + x) for y in spot] for x in spot]
+    lines += [[2 * (y * side + x) + 1 for x in spot] for y in spot]
+    beside = [
+        (line[i], line[i ^ 1])
+        for line in lines
+        for i in spot
+        if (line[i] // 2 // side + line[i] // 2 % side) % 2 == line[i] % 2
+    ]
     swap = [(0, 1), (1, 0)]
     core = lax.axis_index("ba")
     bank = lax.axis_index("aa")
     column, line = bank % side, bank // side
-    position = jnp.where(core == 0, column, line)
+    position = jnp.where(core == 0, line, column)
     flag = core.astype(jnp.int32).reshape(1)
-
+    at = jnp.stack([core, position % 2, (column + line) % 2]).astype(jnp.int32)
+
+    piece = jax.ShapeDtypeStruct((3 * half, half_model), jnp.bfloat16)
+    ours, theirs = call(
+        functools.partial(cut_kernel, half),
+        [at, adapter_down_matrix[0].T, adapter_up_matrix[0]],
+        [piece, piece],
+        0,
+    )
+    theirs = lax.ppermute(theirs, both, beside)
     far_hidden = lax.ppermute(hidden, "ba", swap)
-
-    halves = adapter_down_matrix[0].T.reshape(2, half, 2, half_model)
-    whole = jnp.concatenate(
+    near, slot = call(
+        functools.partial(near_kernel, side),
+        [at, tenant_adapter_index.reshape(1, requests), hidden],
         [
-            jnp.where(core == 0, halves[:, :, 1], halves[:, :, 0]),
-            jnp.where(core == 0, halves[:, :, 0], halves[:, :, 1]),
-            adapter_up_matrix[0].reshape(2, half, width_query),
-        ],
-        axis=1,
-    )
-    odd = position % 2 == 1
-    ours = jnp.where(odd, whole[1], whole[0])
-    theirs = lax.ppermute(jnp.where(odd, whole[0], whole[1]), both, beside)
-    sent_bank = jnp.where((column + line) % 2 == 1 - core, ours, theirs)
-
-    packed, slot = call(
-        functools.partial(pack_kernel, side),
-        [flag, tenant_adapter_index.reshape(1, requests), hidden, far_hidden, sent_bank],
-        [
-            jax.ShapeDtypeStruct((side, 2 * held + 3 * half, half_model), jnp.bfloat16),
+            jax.ShapeDtypeStruct((side * held, half_model), jnp.bfloat16),
             jax.ShapeDtypeStruct((8, requests), jnp.int32),
         ],
-        "pack",
-        4 * side * held * requests * half_model,
+        2 * side * held * requests * half_model,
+    )
+    packed = call(
+        functools.partial(far_kernel, side),
+        [at, slot, near, far_hidden, ours, theirs],
+        jax.ShapeDtypeStruct((side, 2 * held + 3 * half, half_model), jnp.bfloat16),
+        2 * side * held * requests * half_model,
     )
     received = lax.all_to_all(packed, both, 0, 0, axis_index_groups=lines, tiled=True)
 
@@ -258,7 +302,6 @@
         functools.partial(raise_kernel, side, rank),
         [received, bank_rows],
         jax.ShapeDtypeStruct((side, held, width_query), jnp.bfloat16),
-        "raise",
         6 * side * held * side * half * half_model,
     )
     back = lax.all_to_all(raised, both, 0, 0, axis_index_groups=lines, tiled=True)
@@ -291,7 +334,6 @@
             valid,
         ],
         jax.ShapeDtypeStruct((here, width_query), jnp.bfloat16),
-        "attend",
         4 * here * width_query * tokens * CHUNK,
     )
 

time: 85.4 us -> 83.4 us (0.977)
  starting transfers between devices: 35.2 us -> 29.2 us
  waiting for transfers between devices: 11.2 us -> 13.8 us
  Pallas kernels: 12.8 us -> 14.7 us
  other arithmetic: 1.06 us -> 0.16 us
    ppermute x1, starting transfers between devices: 6.24 us -> 1.88 us  [on_device(): bank_rows = lax.ppermute(received[:, 2 * held:], 'ba', swap)]
    ppermute x1, starting transfers between devices: 17.2 us -> 20.4 us  [on_device(): far_hidden = lax.ppermute(hidden, 'ba', swap)]
    all_to_all x1, waiting for transfers between devices: 6.39 us -> 9.3 us  [on_device(): lax.all_to_all(packed, both, 0, 0, axis_index_groups=lines, tiled=True)]
    ppermute x1, starting transfers between devices: 2.88 us -> 0.14 us  [on_device(): got = lax.ppermute(sent, 'ba', swap)]
    ppermute x1, starting transfers between devices: 3.44 us -> 1.31 us  [on_device(): theirs = lax.ppermute(theirs, both, beside)]
    pallas_call x3 -> x5, Pallas kernels: 3.61 us -> 5.44 us  [call(): pl.pallas_call(kernel, out_shape=out, in_specs=specs, out_specs=jax.tree....]
    ppermute x1, waiting for transfers between devices: 1.72 us -> 0.01 us  [on_device(): far_hidden = lax.ppermute(hidden, 'ba', swap)]
    unnamed x20 -> x24, local copies, waits for them, and re-layouts: 8.23 us -> 9.95 us
  transfers between devices with their start and end apart: 6 -> 6, of which waited for: 4 -> 4; matrix products, arithmetic and copies ran while one was open for 1% -> 1% of each run, Pallas kernels for 10% -> 12%
where the time goes in v3:
time: 83.4 us; the launch traced here: 82.9 us
  starting transfers between devices  29.2 us (35%)
  Pallas kernels  14.7 us (18%)
  blocking collectives  14.6 us (18%)
  waiting for transfers between devices  13.8 us (17%)
  local copies, waits for them, and re-layouts  10.3 us (12%)
    ppermute x1, starting transfers between devices, on_device(): far_hidden = lax.ppermute(hidden, 'ba', swap)  20.4 us
    all_to_all x1, blocking collectives, on_device(): lax.all_to_all(raised, both, 0, 0, axis_index_groups=lines, tiled=True)  14.6 us
    unnamed x24, local copies, waits for them, and re-layouts  9.95 us
    all_to_all x1, waiting for transfers between devices, on_device(): lax.all_to_all(packed, both, 0, 0, axis_index_groups=lines, tiled=True)  9.3 us
    pallas_call x1, Pallas kernels, project(): pl.pallas_call(functools.partial(project_kernel, kvw // size, size), grid...  8.84 us
    pallas_call x5, Pallas kernels, call(): pl.pallas_call(kernel, out_shape=out, in_specs=specs, out_specs=jax.tree....  5.44 us
    all_to_all x1, starting transfers between devices, on_device(): lax.all_to_all(packed, both, 0, 0, axis_index_groups=lines, tiled=True)  3.8 us
    ppermute x1, waiting for transfers between devices, on_device(): bank_rows = lax.ppermute(received[:, 2 * held:], 'ba', swap)  1.91 us
  transfers between devices with their start and end apart: 6, of which 4 were waited for; matrix products, arithmetic and copies ran while one was open for 1% of the time, Pallas kernels for 12%

profile of v3, /device:TPU:513, one launch (start us, length us, event | category | flops | bytes accessed | tf_op | source)
XLA Modules:
  0.0 82.9 jit_solution(12154246916610374697)
XLA Ops:
  0.0 0.0 copy-start.11
  0.0 0.0 copy-start.9
  0.0 20.4 %collective-permute-start = (bf16[128,2048]{1,0:T(8,128)(2,1)}, bf16[128,2048]{1,0:T(8,128)(2,1)S(1)}, u32[]{:S(2)}, u32[]{:S(2)}) collective-permute-start(bf16[128,2048]{1,0:T(8,128)(2,1)} %mine_ref.1), channel_id=1, source_target_pairs={{0,1},{1,0},{2,3},{3,2},{4,5},{5,4},{6,7},{7,6},{8,9},{9,8},{10,11... | collective-permute-start | bytes 1572872 | tf_op jit(solution)/shard_map/ppermute | solution.py:267
  20.4 0.1 pad_add_fusion.at_ref
  20.5 0.0 copy-start.4
  20.5 0.9 %copy-done.4 = bf16[1,4096,16]{1,2,0:T(8,128)(2,1)S(1)} copy-done((bf16[1,4096,16]{1,2,0:T(8,128)(2,1)S(1)}, bf16[1,4096,16]{1,2,0:T(8,128)(2,1)}, u32[]{:S(2)}) %copy-start.4) | copy-done | bytes 131096
  21.4 0.0 copy-start.5
  21.4 0.8 %copy-done.5 = bf16[1,16,2048]{2,1,0:T(8,128)(2,1)S(1)} copy-done((bf16[1,16,2048]{2,1,0:T(8,128)(2,1)S(1)}, bf16[1,16,2048]{2,1,0:T(8,128)(2,1)}, u32[]{:S(2)}) %copy-start.5) | copy-done | bytes 65560
  22.2 0.6 shard_map.101
  22.8 1.3 %collective-permute-start.1 = (bf16[24,2048]{1,0:T(8,128)(2,1)S(1)}, bf16[24,2048]{1,0:T(8,128)(2,1)S(1)}, u32[]{:S(2)}, u32[]{:S(2)}) collective-permute-start(bf16[24,2048]{1,0:T(8,128)(2,1)S(1)} %get-tuple-element.21), channel_id=1, source_target_pairs={{0,16},{32,48},{64,80},{96,112},{18,2},{50,34},{82,66},{114,98},{4... | collective-permute-start | bytes 294920 | tf_op jit(solution)/shard_map/ppermute | solution.py:266
  24.1 0.0 copy-start.3
  24.1 1.0 %copy-done.3 = bf16[128,2048]{1,0:T(8,128)(2,1)S(1)} copy-done((bf16[128,2048]{1,0:T(8,128)(2,1)S(1)}, bf16[128,2048]{1,0:T(8,128)(2,1)}, u32[]{:S(2)}) %copy-start.3) | copy-done | bytes 524312
  25.2 0.0 copy-start.6
  25.2 0.7 copy-done.6
  25.8 0.9 %shard_map.100 = (bf16[128,2048]{1,0:T(8,128)(2,1)S(1)}, s32[8,128]{1,0:T(8,128)S(1)}) custom-call(s32[3]{0:T(128)S(1)} %pad_add_fusion.at_ref, s32[1,128]{1,0:T(1,128)S(1)} %bitcast.20, bf16[128,2048]{1,0:T(8,128)(2,1)S(1)} %copy-done.3), custom_call_target="tpu_custom_call" | custom-call | flops 67108864 | bytes 1053196 | tf_op jit(solution)/shard_map/pallas_call | solution.py:21
  26.8 1.4 %collective-permute-done.1.theirs_ref = bf16[24,2048]{1,0:T(8,128)(2,1)S(1)} collective-permute-done((bf16[24,2048]{1,0:T(8,128)(2,1)S(1)}, bf16[24,2048]{1,0:T(8,128)(2,1)S(1)}, u32[]{:S(2)}, u32[]{:S(2)}) %collective-permute-start.1) | collective-permute-done | bytes 98336 | tf_op jit(solution)/shard_map/ppermute | solution.py:266
  28.2 0.0 collective-permute-done.other_ref
  28.2 0.9 %shard_map.102 = bf16[8,56,2048]{2,1,0:T(8,128)(2,1)S(1)} custom-call(s32[3]{0:T(128)S(1)} %pad_add_fusion.at_ref, s32[8,128]{1,0:T(8,128)S(1)} %get-tuple-element.18.slot_ref, bf16[128,2048]{1,0:T(8,128)(2,1)S(1)} %get-tuple-element.19.near_ref, bf16[128,2048]{1,0:T(8,128)(2,1)S(1)} %collective-permute-done.other_ref, ...), custom_call_target="tpu_custom_call" | custom-call | flops 67108864 | bytes 3084300 | tf_op jit(solution)/shard_map/pallas_call | solution.py:21
  29.1 0.0 copy-start
  29.1 1.3 %copy-done = bf16[8,56,2048]{2,1,0:T(8,128)(2,1)} copy-done((bf16[8,56,2048]{2,1,0:T(8,128)(2,1)}, bf16[8,56,2048]{2,1,0:T(8,128)(2,1)S(1)}, u32[]{:S(2)}) %copy-start) | copy-done | bytes 1835032
  30.4 3.8 %all-to-all-start = ((bf16[8,56,2048]{2,1,0:T(8,128)(2,1)}), bf16[8,56,2048]{2,1,0:T(8,128)(2,1)S(1)}, u32[]{:S(2)}, u32[]{:S(2)}) async-start(bf16[8,56,2048]{2,1,0:T(8,128)(2,1)} %copy-done), calls=%async_computation | async-start | bytes 3670016 | tf_op jit(solution)/shard_map/all_to_all | solution.py:283
  34.2 0.0 copy-done.10
  34.2 0.1 collective-permute-start.2
  34.3 0.0 copy-done.11
  34.4 0.1 lt.50
  34.4 0.1 lt.47
  34.5 0.1 lt.48
  34.6 0.1 lt.52
  34.7 0.0 copy-done.9
  34.7 0.0 copy-start.7
  34.7 2.2 %copy-done.7 = bf16[4096,512]{1,0:T(8,128)(2,1)S(1)} copy-done((bf16[4096,512]{1,0:T(8,128)(2,1)S(1)}, bf16[4096,512]{1,0:T(8,128)(2,1)}, u32[]{:S(2)}) %copy-start.7) | copy-done | bytes 4194328
  36.9 2.2 %copy-done.8 = bf16[4096,512]{1,0:T(8,128)(2,1)S(1)} copy-done((bf16[4096,512]{1,0:T(8,128)(2,1)S(1)}, bf16[4096,512]{1,0:T(8,128)(2,1)}, u32[]{:S(2)}) %copy-start.8) | copy-done | bytes 4194328
  39.1 8.8 %project.1 = (bf16[768,512]{1,0:T(8,128)(2,1)S(1)}, bf16[768,512]{1,0:T(8,128)(2,1)S(1)}) custom-call(bf16[768,4096]{1,0:T(8,128)(2,1)} %bitcast.22, bf16[4096,512]{1,0:T(8,128)(2,1)S(1)} %copy-done.7, bf16[4096,512]{1,0:T(8,128)(2,1)S(1)} %copy-done.8, f32[1,128]{1,0:T(1,128)S(1)} %bitcast.21), custom_call_target="tpu_custom_call" | custom-call | flops 6442450944 | bytes 16252928 | tf_op jit(solution)/shard_map/project/pallas_call | solution.py:51
  47.9 0.0 copy-start.1
  47.9 0.9 %copy-done.1 = bf16[768,512]{1,0:T(8,128)(2,1)} copy-done((bf16[768,512]{1,0:T(8,128)(2,1)}, bf16[768,512]{1,0:T(8,128)(2,1)S(1)}, u32[]{:S(2)}) %copy-start.1) | copy-done | bytes 786456
  48.8 0.0 collective-permute-done.2
  48.8 0.1 broadcast_select_fusion.1
  48.9 9.3 %all-to-all-done.rows_ref = bf16[8,56,2048]{2,1,0:T(8,128)(2,1)S(1)} async-done(((bf16[8,56,2048]{2,1,0:T(8,128)(2,1)}), bf16[8,56,2048]{2,1,0:T(8,128)(2,1)S(1)}, u32[]{:S(2)}, u32[]{:S(2)}) %all-to-all-start) | async-done | bytes 1835040 | tf_op jit(solution)/shard_map/all_to_all | solution.py:283
  58.2 0.1 slice.3
  58.3 1.9 %collective-permute-start.3 = (bf16[8,24,2048]{2,1,0:T(8,128)(2,1)S(1)}, bf16[8,24,2048]{2,1,0:T(8,128)(2,1)S(1)}, u32[]{:S(2)}, u32[]{:S(2)}) collective-permute-start(bf16[8,24,2048]{2,1,0:T(8,128)(2,1)S(1)} %slice.3), channel_id=1, source_target_pairs={{0,1},{1,0},{2,3},{3,2},{4,5},{5,4},{6,7},{7,6},{8,9},{9,8},{10,11... | collective-permute-start | bytes 2359304 | tf_op jit(solution)/shard_map/ppermute | solution.py:300
  60.1 1.9 %collective-permute-done.3.bank_ref = bf16[8,24,2048]{2,1,0:T(8,128)(2,1)S(1)} collective-permute-done((bf16[8,24,2048]{2,1,0:T(8,128)(2,1)S(1)}, bf16[8,24,2048]{2,1,0:T(8,128)(2,1)S(1)}, u32[]{:S(2)}, u32[]{:S(2)}) %collective-permute-start.3) | collective-permute-done | bytes 786464 | tf_op jit(solution)/shard_map/ppermute | solution.py:300
  62.0 0.9 %shard_map.103 = bf16[8,16,2048]{2,1,0:T(8,128)(2,1)S(1)} custom-call(bf16[8,56,2048]{2,1,0:T(8,128)(2,1)S(1)} %all-to-all-done.rows_ref, bf16[8,24,2048]{2,1,0:T(8,128)(2,1)S(1)} %collective-permute-done.3.bank_ref), custom_call_target="tpu_custom_call" | custom-call | flops 100663296 | bytes 3145728 | tf_op jit(solution)/shard_map/pallas_call | solution.py:21
  62.9 14.6 %all_to_all.10 = bf16[8,16,2048]{2,1,0:T(8,128)(2,1)S(1)} all-to-all(bf16[8,16,2048]{2,1,0:T(8,128)(2,1)S(1)} %shard_map.103), channel_id=1, replica_groups={{0,16,32,48,64,80,96,112},{2,18,34,50,66,82,98,114},{4,20,36,52,68,84,1..., dimensions={0} | all-to-all | bytes 1048576 | tf_op jit(solution)/shard_map/all_to_all | solution.py:307
  77.5 0.4 unpack.1
  77.9 1.6 %collective-permute-start.4 = (bf16[64,2048]{1,0:T(8,128)(2,1)S(1)}, bf16[64,2048]{1,0:T(8,128)(2,1)S(1)}, u32[]{:S(2)}, u32[]{:S(2)}) collective-permute-start(bf16[64,2048]{1,0:T(8,128)(2,1)S(1)} %get-tuple-element.26), channel_id=1, source_target_pairs={{0,1},{1,0},{2,3},{3,2},{4,5},{5,4},{6,7},{7,6},{8,9},{9,8},{10,11... | collective-permute-start | bytes 786440 | tf_op jit(solution)/shard_map/ppermute | solution.py:324
  79.5 1.2 %collective-permute-done.4.got_ref = bf16[64,2048]{1,0:T(8,128)(2,1)S(1)} collective-permute-done((bf16[64,2048]{1,0:T(8,128)(2,1)S(1)}, bf16[64,2048]{1,0:T(8,128)(2,1)S(1)}, u32[]{:S(2)}, u32[]{:S(2)}) %collective-permute-start.4) | collective-permute-done | bytes 262176 | tf_op jit(solution)/shard_map/ppermute | solution.py:324
  80.7 0.0 copy-done.2
  80.7 2.2 %shard_map.104 = bf16[64,2048]{1,0:T(8,128)(2,1)} custom-call(bf16[64,2048]{1,0:T(8,128)(2,1)S(1)} %get-tuple-element.25.mine_ref, bf16[64,2048]{1,0:T(8,128)(2,1)S(1)} %collective-permute-done.4.got_ref, bf16[64,2048]{1,0:T(8,128)(2,1)S(1)} %pad_maximum_fusion.base_ref, bf16[12,64,512]{2,1,0:T(8,128)(2,1)S(1)} %bitcast.16, ...), custom_call_target="tpu_custom_call" | custom-call | flops 100663296 | bytes 2624512 | tf_op jit(solution)/shard_map/pallas_call | solution.py:21
  (8 shorter events, 0.1 us)
Async XLA Ops:
  0.0 34.3 %copy-start.11 = (s32[64]{0:T(128)S(1)}, s32[64]{0:T(128)}, u32[]{:S(2)}) copy-start(s32[64]{0:T(128)} %param.19) | copy-start | bytes 772
  0.0 34.7 %copy-start.9 = (f32[128]{0:T(128)S(1)}, f32[128]{0:T(128)}, u32[]{:S(2)}) copy-start(f32[128]{0:T(128)} %param.13) | copy-start | bytes 1540
  0.0 28.2 %collective-permute-start = (bf16[128,2048]{1,0:T(8,128)(2,1)}, bf16[128,2048]{1,0:T(8,128)(2,1)S(1)}, u32[]{:S(2)}, u32[]{:S(2)}) collective-permute-start(bf16[128,2048]{1,0:T(8,128)(2,1)} %mine_ref.1), channel_id=1, source_target_pairs={{0,1},{1,0},{2,3},{3,2},{4,5},{5,4},{6,7},{7,6},{8,9},{9,8},{10,11... | collective-permute-start | bytes 1572872 | tf_op jit(solution)/shard_map/ppermute | solution.py:267
  20.5 0.9 %copy-start.4 = (bf16[1,4096,16]{1,2,0:T(8,128)(2,1)S(1)}, bf16[1,4096,16]{1,2,0:T(8,128)(2,1)}, u32[]{:S(2)}) copy-start(bf16[1,4096,16]{1,2,0:T(8,128)(2,1)} %param.16) | copy-start | bytes 393220
  21.4 0.8 %copy-start.5 = (bf16[1,16,2048]{2,1,0:T(8,128)(2,1)S(1)}, bf16[1,16,2048]{2,1,0:T(8,128)(2,1)}, u32[]{:S(2)}) copy-start(bf16[1,16,2048]{2,1,0:T(8,128)(2,1)} %param.17) | copy-start | bytes 196612
  22.8 5.4 %collective-permute-start.1 = (bf16[24,2048]{1,0:T(8,128)(2,1)S(1)}, bf16[24,2048]{1,0:T(8,128)(2,1)S(1)}, u32[]{:S(2)}, u32[]{:S(2)}) collective-permute-start(bf16[24,2048]{1,0:T(8,128)(2,1)S(1)} %get-tuple-element.21), channel_id=1, source_target_pairs={{0,16},{32,48},{64,80},{96,112},{18,2},{50,34},{82,66},{114,98},{4... | collective-permute-start | bytes 294920 | tf_op jit(solution)/shard_map/ppermute | solution.py:266
  24.1 1.0 %copy-start.3 = (bf16[128,2048]{1,0:T(8,128)(2,1)S(1)}, bf16[128,2048]{1,0:T(8,128)(2,1)}, u32[]{:S(2)}) copy-start(bf16[128,2048]{1,0:T(8,128)(2,1)} %mine_ref.1) | copy-start | bytes 1572868
  25.2 0.7 copy-start.6
  25.8 8.3 %copy-start.10 = (bf16[128,1024]{1,0:T(8,128)(2,1)S(1)}, bf16[128,1024]{1,0:T(8,128)(2,1)}, u32[]{:S(2)}) copy-start(bf16[128,1024]{1,0:T(8,128)(2,1)} %param.15) | copy-start | bytes 786436
  29.1 1.3 %copy-start = (bf16[8,56,2048]{2,1,0:T(8,128)(2,1)}, bf16[8,56,2048]{2,1,0:T(8,128)(2,1)S(1)}, u32[]{:S(2)}) copy-start(bf16[8,56,2048]{2,1,0:T(8,128)(2,1)S(1)} %shard_map.102) | copy-start | bytes 5505028
  30.4 27.8 %all-to-all-start = ((bf16[8,56,2048]{2,1,0:T(8,128)(2,1)}), bf16[8,56,2048]{2,1,0:T(8,128)(2,1)S(1)}, u32[]{:S(2)}, u32[]{:S(2)}) async-start(bf16[8,56,2048]{2,1,0:T(8,128)(2,1)} %copy-done), calls=%async_computation | async-start | bytes 3670016 | tf_op jit(solution)/shard_map/all_to_all | solution.py:283
  34.2 14.6 %collective-permute-start.2 = (bf16[64,1024]{1,0:T(8,128)(2,1)S(1)}, bf16[64,1024]{1,0:T(8,128)(2,1)S(1)}, u32[]{:S(2)}, u32[]{:S(2)}) collective-permute-start(bf16[64,1024]{1,0:T(8,128)(2,1)S(1)} %constant_dynamic-slice_fusion), channel_id=1, source_target_pairs={{0,1},{1,0},{2,3},{3,2},{4,5},{5,4},{6,7},{7,6},{8,9},{9,8},{10,11... | collective-permute-start | bytes 393224 | tf_op jit(solution)/shard_map/ppermute | solution.py:289
  34.7 2.2 %copy-start.7 = (bf16[4096,512]{1,0:T(8,128)(2,1)S(1)}, bf16[4096,512]{1,0:T(8,128)(2,1)}, u32[]{:S(2)}) copy-start(bf16[4096,512]{1,0:T(8,128)(2,1)} %wk_ref.1) | copy-start | bytes 12582916
  36.9 2.2 %copy-start.8 = (bf16[4096,512]{1,0:T(8,128)(2,1)S(1)}, bf16[4096,512]{1,0:T(8,128)(2,1)}, u32[]{:S(2)}) copy-start(bf16[4096,512]{1,0:T(8,128)(2,1)} %wv_ref.1) | copy-start | bytes 12582916
  47.9 0.9 %copy-start.1 = (bf16[768,512]{1,0:T(8,128)(2,1)}, bf16[768,512]{1,0:T(8,128)(2,1)S(1)}, u32[]{:S(2)}) copy-start(bf16[768,512]{1,0:T(8,128)(2,1)S(1)} %get-tuple-element.29) | copy-start | bytes 2359300
  58.2 22.5 %copy-start.2 = (bf16[768,512]{1,0:T(8,128)(2,1)S(1)}, bf16[768,512]{1,0:T(8,128)(2,1)}, u32[]{:S(2)}) copy-start(bf16[768,512]{1,0:T(8,128)(2,1)} %copy-done.1) | copy-start | bytes 2359300
  58.3 3.8 %collective-permute-start.3 = (bf16[8,24,2048]{2,1,0:T(8,128)(2,1)S(1)}, bf16[8,24,2048]{2,1,0:T(8,128)(2,1)S(1)}, u32[]{:S(2)}, u32[]{:S(2)}) collective-permute-start(bf16[8,24,2048]{2,1,0:T(8,128)(2,1)S(1)} %slice.3), channel_id=1, source_target_pairs={{0,1},{1,0},{2,3},{3,2},{4,5},{5,4},{6,7},{7,6},{8,9},{9,8},{10,11... | collective-permute-start | bytes 2359304 | tf_op jit(solution)/shard_map/ppermute | solution.py:300
  77.9 2.8 %collective-permute-start.4 = (bf16[64,2048]{1,0:T(8,128)(2,1)S(1)}, bf16[64,2048]{1,0:T(8,128)(2,1)S(1)}, u32[]{:S(2)}, u32[]{:S(2)}) collective-permute-start(bf16[64,2048]{1,0:T(8,128)(2,1)S(1)} %get-tuple-element.26), channel_id=1, source_target_pairs={{0,1},{1,0},{2,3},{3,2},{4,5},{5,4},{6,7},{7,6},{8,9},{9,8},{10,11... | collective-permute-start | bytes 786440 | tf_op jit(solution)/shard_map/ppermute | solution.py:324

commit v4 on v3

--- a/solution.py
+++ b/solution.py
@@ -69,42 +69,12 @@
     )(x, wk, wv, gain)
 
 
-def cut_kernel(half, at_ref, down_ref, up_ref, ours_ref, theirs_ref):
-    core, odd = at_ref[0], at_ref[1]
-    width = ours_ref.shape[1]
-
-    def cut(out, low):
-        rows = slice(low * half, (low + 1) * half)
-
-        @pl.when(core == 0)
-        def _():
-            out[:half] = down_ref[rows, width:]
-            out[half : 2 * half] = down_ref[rows, :width]
-
-        @pl.when(core != 0)
-        def _():
-            out[:half] = down_ref[rows, :width]
-            out[half : 2 * half] = down_ref[rows, width:]
-
-        out[2 * half :] = up_ref[rows]
-
-    @pl.when(odd == 0)
-    def _():
-        cut(ours_ref, 0)
-        cut(theirs_ref, 1)
-
-    @pl.when(odd != 0)
-    def _():
-        cut(ours_ref, 1)
-        cut(theirs_ref, 0)
-
-
 def placing_of(slot, slots):
     row = lax.broadcasted_iota(jnp.int32, (slots, slot.shape[1]), 0)
     return jnp.where(row == slot, 1.0, 0.0).astype(jnp.bfloat16)
 
 
-def near_kernel(side, at_ref, names_ref, mine_ref, near_ref, slot_ref):
+def slot_kernel(side, at_ref, names_ref, slot_ref):
     requests = names_ref.shape[1]
     held = side // 2 * SLOTS
     core = at_ref[0]
@@ -121,23 +91,39 @@
     which = jnp.where(core == 0, column, line) // 2
     slot = jnp.where((column + line) % 2 == 1 - core, peer * held + which * SLOTS + rank, -1)
     slot_ref[...] = jnp.broadcast_to(slot, slot_ref.shape)
-    placing = placing_of(slot, side * held)
-    near_ref[...] = jnp.dot(placing, mine_ref[...], preferred_element_type=jnp.float32).astype(
-        jnp.bfloat16
-    )
-
-
-def far_kernel(side, at_ref, slot_ref, near_ref, other_ref, ours_ref, theirs_ref, out_ref):
+
+
+def pack_kernel(
+    side, at_ref, slot_ref, mine_ref, other_ref, down_ref, up_ref, next_down_ref, next_up_ref, out_ref
+):
     held = side // 2 * SLOTS
+    core, odd, owned = at_ref[0], at_ref[1], at_ref[2]
+    width = other_ref.shape[1]
+    half = down_ref.shape[0] // 2
+
+    def cut(down, up, low):
+        rows = slice(low * half, (low + 1) * half)
+        left, right = down[rows, :width], down[rows, width:]
+        piece = jnp.concatenate(
+            [jnp.where(core == 0, right, left), jnp.where(core == 0, left, right), up[rows]], axis=0
+        )
+        for p in range(side):
+            out_ref[p, 2 * held :] = piece
+
+    for own, (down, up) in ((1, (down_ref, up_ref)), (0, (next_down_ref, next_up_ref))):
+        for low in (0, 1):
+
+            @pl.when((owned == own) & (odd == low))
+            def _():
+                cut(down, up, low)
+
     placing = placing_of(slot_ref[:1], side * held)
-    other = jnp.dot(placing, other_ref[...], preferred_element_type=jnp.float32).astype(
-        jnp.bfloat16
-    )
-    bank = jnp.where(at_ref[2] == at_ref[0], ours_ref[...], theirs_ref[...])
-    for p in range(side):
-        out_ref[p, :held] = near_ref[p * held : (p + 1) * held]
-        out_ref[p, held : 2 * held] = other[p * held : (p + 1) * held]
-        out_ref[p, 2 * held :] = bank
+    for n, source in enumerate((mine_ref, other_ref)):
+        placed = jnp.dot(placing, source[...], preferred_element_type=jnp.float32).astype(
+            jnp.bfloat16
+        )
+        for p in range(side):
+            out_ref[p, n * held : (n + 1) * held] = placed[p * held : (p + 1) * held]
 
 
 def raise_kernel(side, rank, rows_ref, bank_ref, out_ref):
@@ -243,7 +229,7 @@
     lines = [[2 * (y * side + x) for y in spot] for x in spot]
     lines += [[2 * (y * side + x) + 1 for x in spot] for y in spot]
     beside = [
-        (line[i], line[i ^ 1])
+        (line[i] | 1, line[i ^ 1])
         for line in lines
         for i in spot
         if (line[i] // 2 // side + line[i] // 2 % side) % 2 == line[i] % 2
@@ -254,31 +240,24 @@
     column, line = bank % side, bank // side
     position = jnp.where(core == 0, line, column)
     flag = core.astype(jnp.int32).reshape(1)
-    at = jnp.stack([core, position % 2, (column + line) % 2]).astype(jnp.int32)
-
-    piece = jax.ShapeDtypeStruct((3 * half, half_model), jnp.bfloat16)
-    ours, theirs = call(
-        functools.partial(cut_kernel, half),
-        [at, adapter_down_matrix[0].T, adapter_up_matrix[0]],
-        [piece, piece],
-        0,
-    )
-    theirs = lax.ppermute(theirs, both, beside)
+    owned = (column + line) % 2 == core
+    at = jnp.stack([core, position % 2, owned]).astype(jnp.int32)
+
+    down, up = adapter_down_matrix[0].T, adapter_up_matrix[0]
+    next_down = lax.ppermute(down, both, beside)
+    next_up = lax.ppermute(up, both, beside)
     far_hidden = lax.ppermute(hidden, "ba", swap)
-    near, slot = call(
-        functools.partial(near_kernel, side),
-        [at, tenant_adapter_index.reshape(1, requests), hidden],
-        [
-            jax.ShapeDtypeStruct((side * held, half_model), jnp.bfloat16),
-            jax.ShapeDtypeStruct((8, requests), jnp.int32),
-        ],
-        2 * side * held * requests * half_model,
+    slot = call(
+        functools.partial(slot_kernel, side),
+        [at, tenant_adapter_index.reshape(1, requests)],
+        jax.ShapeDtypeStruct((8, requests), jnp.int32),
+        2 * 10**10,
     )
     packed = call(
-        functools.partial(far_kernel, side),
-        [at, slot, near, far_hidden, ours, theirs],
+        functools.partial(pack_kernel, side),
+        [at, slot, hidden, far_hidden, down, up, next_down, next_up],
         jax.ShapeDtypeStruct((side, 2 * held + 3 * half, half_model), jnp.bfloat16),
-        2 * side * held * requests * half_model,
+        4 * side * held * requests * half_model,
     )
     received = lax.all_to_all(packed, both, 0, 0, axis_index_groups=lines, tiled=True)
 

time: 83.4 us -> 80.7 us (0.968)
  local copies, waits for them, and re-layouts: 10.3 us -> 7.64 us
  starting transfers between devices: 29.2 us -> 31.4 us
  waiting for transfers between devices: 13.8 us -> 12.4 us
    ppermute x1 -> x2, starting transfers between devices: 1.31 us -> 7.69 us  [the longest x1 5.74 us: on_device(): next_up = lax.ppermute(up, both, beside)]
    ppermute x1, starting transfers between devices: 20.4 us -> 14.2 us  [on_device(): far_hidden = lax.ppermute(hidden, 'ba', swap)]
    unnamed x24, local copies, waits for them, and re-layouts: 9.95 us -> 7.25 us
    ppermute x1, starting transfers between devices: 1.88 us -> 3.64 us  [on_device(): bank_rows = lax.ppermute(received[:, 2 * held:], 'ba', swap)]
    ppermute x1 -> x2, waiting for transfers between devices: 1.45 us -> 0.01 us  [the longest x1 0.01 us: on_device(): next_down = lax.ppermute(down, both, beside)]
    pallas_call x5 -> x4, Pallas kernels: 5.44 us -> 4.77 us  [call(): pl.pallas_call(kernel, out_shape=out, in_specs=specs, out_specs=jax.tree....]
  transfers between devices with their start and end apart: 6 -> 7, of which waited for: 4 -> 4; matrix products, arithmetic and copies ran while one was open for 1% -> 1% of each run, Pallas kernels for 12% -> 12%
where the time goes in v4:
time: 80.7 us; the launch traced here: 80.3 us
  starting transfers between devices  31.4 us (39%)
  blocking collectives  14.6 us (18%)
  Pallas kernels  14 us (17%)
  waiting for transfers between devices  12.4 us (15%)
  local copies, waits for them, and re-layouts  7.64 us (9%)
    all_to_all x1, blocking collectives, on_device(): lax.all_to_all(raised, both, 0, 0, axis_index_groups=lines, tiled=True)  14.6 us
    ppermute x1, starting transfers between devices, on_device(): far_hidden = lax.ppermute(hidden, 'ba', swap)  14.2 us
    all_to_all x1, waiting for transfers between devices, on_device(): lax.all_to_all(packed, both, 0, 0, axis_index_groups=lines, tiled=True)  9 us
    pallas_call x1, Pallas kernels, project(): pl.pallas_call(functools.partial(project_kernel, kvw // size, size), grid...  8.83 us
    unnamed x24, local copies, waits for them, and re-layouts  7.25 us
    ppermute x1, starting transfers between devices, on_device(): next_up = lax.ppermute(up, both, beside)  5.74 us
    pallas_call x4, Pallas kernels, call(): pl.pallas_call(kernel, out_shape=out, in_specs=specs, out_specs=jax.tree....  4.77 us
    all_to_all x1, starting transfers between devices, on_device(): lax.all_to_all(packed, both, 0, 0, axis_index_groups=lines, tiled=True)  3.8 us
  transfers between devices with their start and end apart: 7, of which 4 were waited for; matrix products, arithmetic and copies ran while one was open for 1% of the time, Pallas kernels for 12%

profile of v4, /device:TPU:513, one launch (start us, length us, event | category | flops | bytes accessed | tf_op | source)
XLA Modules:
  0.0 80.3 jit_solution(4790016815493233793)
XLA Ops:
  0.0 5.7 %collective-permute-start.2 = (bf16[16,2048]{1,0:T(8,128)(2,1)}, bf16[16,2048]{1,0:T(8,128)(2,1)S(1)}, u32[]{:S(2)}, u32[]{:S(2)}) collective-permute-start(bf16[16,2048]{1,0:T(8,128)(2,1)} %bitcast.20), channel_id=1, source_target_pairs={{1,16},{33,48},{65,80},{97,112},{19,2},{51,34},{83,66},{115,98},{5... | collective-permute-start | bytes 196616 | tf_op jit(solution)/shard_map/ppermute | solution.py:248
  5.7 2.0 %collective-permute-start.1 = (bf16[16,4096]{1,0:T(8,128)(2,1)}, bf16[16,4096]{1,0:T(8,128)(2,1)S(1)}, u32[]{:S(2)}, u32[]{:S(2)}) collective-permute-start(bf16[16,4096]{1,0:T(8,128)(2,1)} %bitcast.18), channel_id=1, source_target_pairs={{1,16},{33,48},{65,80},{97,112},{19,2},{51,34},{83,66},{115,98},{5... | collective-permute-start | bytes 393224 | tf_op jit(solution)/shard_map/ppermute | solution.py:247
  7.7 14.2 %collective-permute-start = (bf16[128,2048]{1,0:T(8,128)(2,1)}, bf16[128,2048]{1,0:T(8,128)(2,1)S(1)}, u32[]{:S(2)}, u32[]{:S(2)}) collective-permute-start(bf16[128,2048]{1,0:T(8,128)(2,1)} %mine_ref.1), channel_id=1, source_target_pairs={{0,1},{1,0},{2,3},{3,2},{4,5},{5,4},{6,7},{7,6},{8,9},{9,8},{10,11... | collective-permute-start | bytes 1572872 | tf_op jit(solution)/shard_map/ppermute | solution.py:249
  21.9 0.1 pad_add_fusion.at_ref
  21.9 0.0 copy-start.8
  22.0 0.7 copy-done.8
  22.6 0.0 copy-start.3
  22.6 0.7 shard_map.100.slot_ref
  23.3 0.0 copy-start.10
  23.3 0.0 copy-start.11
  23.3 0.0 copy-start.9
  23.3 0.0 collective-permute-done.2.next_up_ref
  23.3 0.0 collective-permute-done.1.next_down_ref
  23.3 0.3 collective-permute-done.other_ref
  23.6 0.0 copy-done.3
  23.6 0.0 copy-done.4
  23.7 0.0 copy-done.5
  23.7 1.0 %shard_map.101 = bf16[8,56,2048]{2,1,0:T(8,128)(2,1)S(1)} custom-call(s32[3]{0:T(128)S(1)} %pad_add_fusion.at_ref, s32[8,128]{1,0:T(8,128)S(1)} %shard_map.100.slot_ref, bf16[128,2048]{1,0:T(8,128)(2,1)S(1)} %copy-done.3, bf16[128,2048]{1,0:T(8,128)(2,1)S(1)} %collective-permute-done.other_ref, bf16[16,4096]{1,0:T(8,128)(2,1)S(1)} %bitcast.19, ...), custom_call_target="tpu_custom_call" | custom-call | flops 134217728 | bytes 3280908 | tf_op jit(solution)/shard_map/pallas_call | solution.py:21
  24.7 0.0 copy-start
  24.7 1.3 %copy-done = bf16[8,56,2048]{2,1,0:T(8,128)(2,1)} copy-done((bf16[8,56,2048]{2,1,0:T(8,128)(2,1)}, bf16[8,56,2048]{2,1,0:T(8,128)(2,1)S(1)}, u32[]{:S(2)}) %copy-start) | copy-done | bytes 1835032
  26.0 3.8 %all-to-all-start = ((bf16[8,56,2048]{2,1,0:T(8,128)(2,1)}), bf16[8,56,2048]{2,1,0:T(8,128)(2,1)S(1)}, u32[]{:S(2)}, u32[]{:S(2)}) async-start(bf16[8,56,2048]{2,1,0:T(8,128)(2,1)} %copy-done), calls=%async_computation | async-start | bytes 3670016 | tf_op jit(solution)/shard_map/all_to_all | solution.py:262
  29.8 0.0 copy-done.10
  29.8 0.5 collective-permute-start.3
  30.3 0.0 copy-done.11
  30.3 0.1 lt.50
  30.4 0.1 lt.47
  30.5 0.1 lt.48
  30.5 0.1 lt.52
  30.6 0.0 copy-done.9
  30.6 0.0 copy-start.6
  30.6 2.2 %copy-done.6 = bf16[4096,512]{1,0:T(8,128)(2,1)S(1)} copy-done((bf16[4096,512]{1,0:T(8,128)(2,1)S(1)}, bf16[4096,512]{1,0:T(8,128)(2,1)}, u32[]{:S(2)}) %copy-start.6) | copy-done | bytes 4194328
  32.8 2.2 %copy-done.7 = bf16[4096,512]{1,0:T(8,128)(2,1)S(1)} copy-done((bf16[4096,512]{1,0:T(8,128)(2,1)S(1)}, bf16[4096,512]{1,0:T(8,128)(2,1)}, u32[]{:S(2)}) %copy-start.7) | copy-done | bytes 4194328
  35.0 8.8 %project.1 = (bf16[768,512]{1,0:T(8,128)(2,1)S(1)}, bf16[768,512]{1,0:T(8,128)(2,1)S(1)}) custom-call(bf16[768,4096]{1,0:T(8,128)(2,1)} %bitcast.24, bf16[4096,512]{1,0:T(8,128)(2,1)S(1)} %copy-done.6, bf16[4096,512]{1,0:T(8,128)(2,1)S(1)} %copy-done.7, f32[1,128]{1,0:T(1,128)S(1)} %bitcast.23), custom_call_target="tpu_custom_call" | custom-call | flops 6442450944 | bytes 16252928 | tf_op jit(solution)/shard_map/project/pallas_call | solution.py:51
  43.8 0.0 copy-start.1
  43.9 0.9 %copy-done.1 = bf16[768,512]{1,0:T(8,128)(2,1)} copy-done((bf16[768,512]{1,0:T(8,128)(2,1)}, bf16[768,512]{1,0:T(8,128)(2,1)S(1)}, u32[]{:S(2)}) %copy-start.1) | copy-done | bytes 786456
  44.7 0.0 collective-permute-done.3
  44.7 0.1 broadcast_select_fusion.1
  44.8 9.0 %all-to-all-done.rows_ref = bf16[8,56,2048]{2,1,0:T(8,128)(2,1)S(1)} async-done(((bf16[8,56,2048]{2,1,0:T(8,128)(2,1)}), bf16[8,56,2048]{2,1,0:T(8,128)(2,1)S(1)}, u32[]{:S(2)}, u32[]{:S(2)}) %all-to-all-start) | async-done | bytes 1835040 | tf_op jit(solution)/shard_map/all_to_all | solution.py:262
  53.8 0.1 slice.3
  53.9 3.6 %collective-permute-start.4 = (bf16[8,24,2048]{2,1,0:T(8,128)(2,1)S(1)}, bf16[8,24,2048]{2,1,0:T(8,128)(2,1)S(1)}, u32[]{:S(2)}, u32[]{:S(2)}) collective-permute-start(bf16[8,24,2048]{2,1,0:T(8,128)(2,1)S(1)} %slice.3), channel_id=1, source_target_pairs={{0,1},{1,0},{2,3},{3,2},{4,5},{5,4},{6,7},{7,6},{8,9},{9,8},{10,11... | collective-permute-start | bytes 2359304 | tf_op jit(solution)/shard_map/ppermute | solution.py:279
  57.5 1.9 %collective-permute-done.4.bank_ref = bf16[8,24,2048]{2,1,0:T(8,128)(2,1)S(1)} collective-permute-done((bf16[8,24,2048]{2,1,0:T(8,128)(2,1)S(1)}, bf16[8,24,2048]{2,1,0:T(8,128)(2,1)S(1)}, u32[]{:S(2)}, u32[]{:S(2)}) %collective-permute-start.4) | collective-permute-done | bytes 786464 | tf_op jit(solution)/shard_map/ppermute | solution.py:279
  59.4 0.9 %shard_map.102 = bf16[8,16,2048]{2,1,0:T(8,128)(2,1)S(1)} custom-call(bf16[8,56,2048]{2,1,0:T(8,128)(2,1)S(1)} %all-to-all-done.rows_ref, bf16[8,24,2048]{2,1,0:T(8,128)(2,1)S(1)} %collective-permute-done.4.bank_ref), custom_call_target="tpu_custom_call" | custom-call | flops 100663296 | bytes 3145728 | tf_op jit(solution)/shard_map/pallas_call | solution.py:21
  60.3 14.6 %all_to_all.10 = bf16[8,16,2048]{2,1,0:T(8,128)(2,1)S(1)} all-to-all(bf16[8,16,2048]{2,1,0:T(8,128)(2,1)S(1)} %shard_map.102), channel_id=1, replica_groups={{0,16,32,48,64,80,96,112},{2,18,34,50,66,82,98,114},{4,20,36,52,68,84,1..., dimensions={0} | all-to-all | bytes 1048576 | tf_op jit(solution)/shard_map/all_to_all | solution.py:286
  74.9 0.4 unpack.1
  75.3 1.6 %collective-permute-start.5 = (bf16[64,2048]{1,0:T(8,128)(2,1)S(1)}, bf16[64,2048]{1,0:T(8,128)(2,1)S(1)}, u32[]{:S(2)}, u32[]{:S(2)}) collective-permute-start(bf16[64,2048]{1,0:T(8,128)(2,1)S(1)} %get-tuple-element.18), channel_id=1, source_target_pairs={{0,1},{1,0},{2,3},{3,2},{4,5},{5,4},{6,7},{7,6},{8,9},{9,8},{10,11... | collective-permute-start | bytes 786440 | tf_op jit(solution)/shard_map/ppermute | solution.py:303
  76.9 1.2 %collective-permute-done.5.got_ref = bf16[64,2048]{1,0:T(8,128)(2,1)S(1)} collective-permute-done((bf16[64,2048]{1,0:T(8,128)(2,1)S(1)}, bf16[64,2048]{1,0:T(8,128)(2,1)S(1)}, u32[]{:S(2)}, u32[]{:S(2)}) %collective-permute-start.5) | collective-permute-done | bytes 262176 | tf_op jit(solution)/shard_map/ppermute | solution.py:303
  78.1 0.0 copy-done.2
  78.1 2.2 %shard_map.103 = bf16[64,2048]{1,0:T(8,128)(2,1)} custom-call(bf16[64,2048]{1,0:T(8,128)(2,1)S(1)} %get-tuple-element.17.mine_ref, bf16[64,2048]{1,0:T(8,128)(2,1)S(1)} %collective-permute-done.5.got_ref, bf16[64,2048]{1,0:T(8,128)(2,1)S(1)} %pad_maximum_fusion.base_ref, bf16[12,64,512]{2,1,0:T(8,128)(2,1)S(1)} %bitcast.16, ...), custom_call_target="tpu_custom_call" | custom-call | flops 100663296 | bytes 2624512 | tf_op jit(solution)/shard_map/pallas_call | solution.py:21
  (9 shorter events, 0.1 us)
Async XLA Ops:
  0.0 23.3 %collective-permute-start.2 = (bf16[16,2048]{1,0:T(8,128)(2,1)}, bf16[16,2048]{1,0:T(8,128)(2,1)S(1)}, u32[]{:S(2)}, u32[]{:S(2)}) collective-permute-start(bf16[16,2048]{1,0:T(8,128)(2,1)} %bitcast.20), channel_id=1, source_target_pairs={{1,16},{33,48},{65,80},{97,112},{19,2},{51,34},{83,66},{115,98},{5... | collective-permute-start | bytes 196616 | tf_op jit(solution)/shard_map/ppermute | solution.py:248
  5.7 17.6 %collective-permute-start.1 = (bf16[16,4096]{1,0:T(8,128)(2,1)}, bf16[16,4096]{1,0:T(8,128)(2,1)S(1)}, u32[]{:S(2)}, u32[]{:S(2)}) collective-permute-start(bf16[16,4096]{1,0:T(8,128)(2,1)} %bitcast.18), channel_id=1, source_target_pairs={{1,16},{33,48},{65,80},{97,112},{19,2},{51,34},{83,66},{115,98},{5... | collective-permute-start | bytes 393224 | tf_op jit(solution)/shard_map/ppermute | solution.py:247
  7.7 15.9 %collective-permute-start = (bf16[128,2048]{1,0:T(8,128)(2,1)}, bf16[128,2048]{1,0:T(8,128)(2,1)S(1)}, u32[]{:S(2)}, u32[]{:S(2)}) collective-permute-start(bf16[128,2048]{1,0:T(8,128)(2,1)} %mine_ref.1), channel_id=1, source_target_pairs={{0,1},{1,0},{2,3},{3,2},{4,5},{5,4},{6,7},{7,6},{8,9},{9,8},{10,11... | collective-permute-start | bytes 1572872 | tf_op jit(solution)/shard_map/ppermute | solution.py:249
  21.9 0.7 copy-start.8
  22.6 1.0 %copy-start.3 = (bf16[128,2048]{1,0:T(8,128)(2,1)S(1)}, bf16[128,2048]{1,0:T(8,128)(2,1)}, u32[]{:S(2)}) copy-start(bf16[128,2048]{1,0:T(8,128)(2,1)} %mine_ref.1) | copy-start | bytes 1572868
  22.6 1.1 %copy-start.4 = (bf16[1,4096,16]{1,2,0:T(8,128)(2,1)S(1)}, bf16[1,4096,16]{1,2,0:T(8,128)(2,1)}, u32[]{:S(2)}) copy-start(bf16[1,4096,16]{1,2,0:T(8,128)(2,1)} %param.16) | copy-start | bytes 393220
  22.6 1.1 %copy-start.5 = (bf16[1,16,2048]{2,1,0:T(8,128)(2,1)S(1)}, bf16[1,16,2048]{2,1,0:T(8,128)(2,1)}, u32[]{:S(2)}) copy-start(bf16[1,16,2048]{2,1,0:T(8,128)(2,1)} %param.17) | copy-start | bytes 196612
  23.3 6.5 %copy-start.10 = (bf16[128,1024]{1,0:T(8,128)(2,1)S(1)}, bf16[128,1024]{1,0:T(8,128)(2,1)}, u32[]{:S(2)}) copy-start(bf16[128,1024]{1,0:T(8,128)(2,1)} %param.15) | copy-start | bytes 786436
  23.3 7.0 %copy-start.11 = (s32[64]{0:T(128)S(1)}, s32[64]{0:T(128)}, u32[]{:S(2)}) copy-start(s32[64]{0:T(128)} %param.19) | copy-start | bytes 772
  23.3 7.3 %copy-start.9 = (f32[128]{0:T(128)S(1)}, f32[128]{0:T(128)}, u32[]{:S(2)}) copy-start(f32[128]{0:T(128)} %param.13) | copy-start | bytes 1540
  24.7 1.3 %copy-start = (bf16[8,56,2048]{2,1,0:T(8,128)(2,1)}, bf16[8,56,2048]{2,1,0:T(8,128)(2,1)S(1)}, u32[]{:S(2)}) copy-start(bf16[8,56,2048]{2,1,0:T(8,128)(2,1)S(1)} %shard_map.101) | copy-start | bytes 5505028
  26.0 27.8 %all-to-all-start = ((bf16[8,56,2048]{2,1,0:T(8,128)(2,1)}), bf16[8,56,2048]{2,1,0:T(8,128)(2,1)S(1)}, u32[]{:S(2)}, u32[]{:S(2)}) async-start(bf16[8,56,2048]{2,1,0:T(8,128)(2,1)} %copy-done), calls=%async_computation | async-start | bytes 3670016 | tf_op jit(solution)/shard_map/all_to_all | solution.py:262
  29.8 14.9 %collective-permute-start.3 = (bf16[64,1024]{1,0:T(8,128)(2,1)S(1)}, bf16[64,1024]{1,0:T(8,128)(2,1)S(1)}, u32[]{:S(2)}, u32[]{:S(2)}) collective-permute-start(bf16[64,1024]{1,0:T(8,128)(2,1)S(1)} %constant_dynamic-slice_fusion), channel_id=1, source_target_pairs={{0,1},{1,0},{2,3},{3,2},{4,5},{5,4},{6,7},{7,6},{8,9},{9,8},{10,11... | collective-permute-start | bytes 393224 | tf_op jit(solution)/shard_map/ppermute | solution.py:268
  30.6 2.2 %copy-start.6 = (bf16[4096,512]{1,0:T(8,128)(2,1)S(1)}, bf16[4096,512]{1,0:T(8,128)(2,1)}, u32[]{:S(2)}) copy-start(bf16[4096,512]{1,0:T(8,128)(2,1)} %wk_ref.1) | copy-start | bytes 12582916
  32.8 2.2 %copy-start.7 = (bf16[4096,512]{1,0:T(8,128)(2,1)S(1)}, bf16[4096,512]{1,0:T(8,128)(2,1)}, u32[]{:S(2)}) copy-start(bf16[4096,512]{1,0:T(8,128)(2,1)} %wv_ref.1) | copy-start | bytes 12582916
  43.8 0.9 %copy-start.1 = (bf16[768,512]{1,0:T(8,128)(2,1)}, bf16[768,512]{1,0:T(8,128)(2,1)S(1)}, u32[]{:S(2)}) copy-start(bf16[768,512]{1,0:T(8,128)(2,1)S(1)} %get-tuple-element.21) | copy-start | bytes 2359300
  53.8 24.3 %copy-start.2 = (bf16[768,512]{1,0:T(8,128)(2,1)S(1)}, bf16[768,512]{1,0:T(8,128)(2,1)}, u32[]{:S(2)}) copy-start(bf16[768,512]{1,0:T(8,128)(2,1)} %copy-done.1) | copy-start | bytes 2359300
  53.9 5.5 %collective-permute-start.4 = (bf16[8,24,2048]{2,1,0:T(8,128)(2,1)S(1)}, bf16[8,24,2048]{2,1,0:T(8,128)(2,1)S(1)}, u32[]{:S(2)}, u32[]{:S(2)}) collective-permute-start(bf16[8,24,2048]{2,1,0:T(8,128)(2,1)S(1)} %slice.3), channel_id=1, source_target_pairs={{0,1},{1,0},{2,3},{3,2},{4,5},{5,4},{6,7},{7,6},{8,9},{9,8},{10,11... | collective-permute-start | bytes 2359304 | tf_op jit(solution)/shard_map/ppermute | solution.py:279
  75.3 2.8 %collective-permute-start.5 = (bf16[64,2048]{1,0:T(8,128)(2,1)S(1)}, bf16[64,2048]{1,0:T(8,128)(2,1)S(1)}, u32[]{:S(2)}, u32[]{:S(2)}) collective-permute-start(bf16[64,2048]{1,0:T(8,128)(2,1)S(1)} %get-tuple-element.18), channel_id=1, source_target_pairs={{0,1},{1,0},{2,3},{3,2},{4,5},{5,4},{6,7},{7,6},{8,9},{9,8},{10,11... | collective-permute-start | bytes 786440 | tf_op jit(solution)/shard_map/ppermute | solution.py:303

commit v5 on v4

--- a/solution.py
+++ b/solution.py
@@ -171,11 +171,12 @@
     same = (row % CHUNK) == (col % CHUNK)
     delta = mine_ref[...].astype(jnp.float32) + got_ref[...].astype(jnp.float32)
     query = (base_ref[...].astype(jnp.float32) + delta).astype(jnp.bfloat16)
-    for c in range(requests // CHUNK):
-        rows = slice(c * CHUNK, (c + 1) * CHUNK)
-        use = same & (valid_ref[c : c + 1, :] > 0.0)
+    scale = 1.0 / math.sqrt(size)
+    for c in range(0, requests // CHUNK, 2):
+        jobs = [(c + n, h) for n in range(2) for h in range(heads)]
         scores = []
-        for h in range(heads):
+        for n, h in jobs:
+            rows = slice(n * CHUNK, (n + 1) * CHUNK)
             q = jnp.concatenate(
                 [
                     query[rows, (h * group + g) * size : (h * group + g + 1) * size]
@@ -186,19 +187,21 @@
             k = k_ref[:, rows, h * size : (h + 1) * size].reshape(wide, size)
             scores.append(
                 lax.dot_general(q, k, (((1,), (1,)), ((), ())), preferred_element_type=jnp.float32)
-                / math.sqrt(size)
             )
         done = []
-        for h in range(heads):
-            masked = jnp.where(use, scores[h], -jnp.inf)
+        for (n, h), score in zip(jobs, scores):
+            rows = slice(n * CHUNK, (n + 1) * CHUNK)
+            use = same & (valid_ref[n : n + 1, :] > 0.0)
+            masked = jnp.where(use, score * scale, -jnp.inf)
             weights = jnp.exp(masked - jnp.max(masked, axis=-1, keepdims=True))
             total = jnp.sum(weights, axis=-1, keepdims=True)
             v = v_ref[:, rows, h * size : (h + 1) * size].reshape(wide, size)
             weighted = jnp.dot(weights.astype(jnp.bfloat16), v, preferred_element_type=jnp.float32)
-            done.append((weighted / total).astype(jnp.bfloat16))
-        for h in range(heads):
+            done.append((weighted * (1.0 / total)).astype(jnp.bfloat16))
+        for (n, h), part in zip(jobs, done):
+            rows = slice(n * CHUNK, (n + 1) * CHUNK)
             for g in range(group):
-                out_ref[rows, (h * group + g) * size : (h * group + g + 1) * size] = done[h][
+                out_ref[rows, (h * group + g) * size : (h * group + g + 1) * size] = part[
                     g * CHUNK : (g + 1) * CHUNK
                 ]
 

time: 80.7 us -> 80.3 us (level)
  no operation moved by 1% of the time
where the time goes in v5:
time: 80.3 us; the launch traced here: 79.9 us
  starting transfers between devices  31.4 us (39%)
  blocking collectives  14.6 us (18%)
  Pallas kernels  13.6 us (17%)
  waiting for transfers between devices  12.4 us (15%)
  local copies, waits for them, and re-layouts  7.64 us (10%)
    all_to_all x1, blocking collectives, on_device(): lax.all_to_all(raised, both, 0, 0, axis_index_groups=lines, tiled=True)  14.6 us
    ppermute x1, starting transfers between devices, on_device(): far_hidden = lax.ppermute(hidden, 'ba', swap)  14.2 us
    all_to_all x1, waiting for transfers between devices, on_device(): lax.all_to_all(packed, both, 0, 0, axis_index_groups=lines, tiled=True)  9 us
    pallas_call x1, Pallas kernels, project(): pl.pallas_call(functools.partial(project_kernel, kvw // size, size), grid...  8.83 us
    unnamed x24, local copies, waits for them, and re-layouts  7.25 us
    ppermute x1, starting transfers between devices, on_device(): next_up = lax.ppermute(up, both, beside)  5.74 us
    pallas_call x4, Pallas kernels, call(): pl.pallas_call(kernel, out_shape=out, in_specs=specs, out_specs=jax.tree....  4.38 us
    all_to_all x1, starting transfers between devices, on_device(): lax.all_to_all(packed, both, 0, 0, axis_index_groups=lines, tiled=True)  3.8 us
  transfers between devices with their start and end apart: 7, of which 4 were waited for; matrix products, arithmetic and copies ran while one was open for 1% of the time, Pallas kernels for 12%

profile of v5, /device:TPU:513, one launch (start us, length us, event | category | flops | bytes accessed | tf_op | source)
XLA Modules:
  0.0 79.9 jit_solution(12858491253085763395)
XLA Ops:
  0.0 5.7 %collective-permute-start.2 = (bf16[16,2048]{1,0:T(8,128)(2,1)}, bf16[16,2048]{1,0:T(8,128)(2,1)S(1)}, u32[]{:S(2)}, u32[]{:S(2)}) collective-permute-start(bf16[16,2048]{1,0:T(8,128)(2,1)} %bitcast.20), channel_id=1, source_target_pairs={{1,16},{33,48},{65,80},{97,112},{19,2},{51,34},{83,66},{115,98},{5... | collective-permute-start | bytes 196616 | tf_op jit(solution)/shard_map/ppermute | solution.py:251
  5.7 2.0 %collective-permute-start.1 = (bf16[16,4096]{1,0:T(8,128)(2,1)}, bf16[16,4096]{1,0:T(8,128)(2,1)S(1)}, u32[]{:S(2)}, u32[]{:S(2)}) collective-permute-start(bf16[16,4096]{1,0:T(8,128)(2,1)} %bitcast.18), channel_id=1, source_target_pairs={{1,16},{33,48},{65,80},{97,112},{19,2},{51,34},{83,66},{115,98},{5... | collective-permute-start | bytes 393224 | tf_op jit(solution)/shard_map/ppermute | solution.py:250
  7.7 14.2 %collective-permute-start = (bf16[128,2048]{1,0:T(8,128)(2,1)}, bf16[128,2048]{1,0:T(8,128)(2,1)S(1)}, u32[]{:S(2)}, u32[]{:S(2)}) collective-permute-start(bf16[128,2048]{1,0:T(8,128)(2,1)} %mine_ref.1), channel_id=1, source_target_pairs={{0,1},{1,0},{2,3},{3,2},{4,5},{5,4},{6,7},{7,6},{8,9},{9,8},{10,11... | collective-permute-start | bytes 1572872 | tf_op jit(solution)/shard_map/ppermute | solution.py:252
  21.9 0.1 pad_add_fusion.at_ref
  21.9 0.0 copy-start.8
  22.0 0.7 copy-done.8
  22.6 0.0 copy-start.3
  22.6 0.7 shard_map.100.slot_ref
  23.3 0.0 copy-start.10
  23.3 0.0 copy-start.11
  23.3 0.0 copy-start.9
  23.3 0.0 collective-permute-done.2.next_up_ref
  23.3 0.0 collective-permute-done.1.next_down_ref
  23.3 0.3 collective-permute-done.other_ref
  23.6 0.0 copy-done.3
  23.6 0.0 copy-done.4
  23.7 0.0 copy-done.5
  23.7 1.0 %shard_map.101 = bf16[8,56,2048]{2,1,0:T(8,128)(2,1)S(1)} custom-call(s32[3]{0:T(128)S(1)} %pad_add_fusion.at_ref, s32[8,128]{1,0:T(8,128)S(1)} %shard_map.100.slot_ref, bf16[128,2048]{1,0:T(8,128)(2,1)S(1)} %copy-done.3, bf16[128,2048]{1,0:T(8,128)(2,1)S(1)} %collective-permute-done.other_ref, bf16[16,4096]{1,0:T(8,128)(2,1)S(1)} %bitcast.19, ...), custom_call_target="tpu_custom_call" | custom-call | flops 134217728 | bytes 3280908 | tf_op jit(solution)/shard_map/pallas_call | solution.py:21
  24.7 0.0 copy-start
  24.7 1.3 %copy-done = bf16[8,56,2048]{2,1,0:T(8,128)(2,1)} copy-done((bf16[8,56,2048]{2,1,0:T(8,128)(2,1)}, bf16[8,56,2048]{2,1,0:T(8,128)(2,1)S(1)}, u32[]{:S(2)}) %copy-start) | copy-done | bytes 1835032
  26.0 3.8 %all-to-all-start = ((bf16[8,56,2048]{2,1,0:T(8,128)(2,1)}), bf16[8,56,2048]{2,1,0:T(8,128)(2,1)S(1)}, u32[]{:S(2)}, u32[]{:S(2)}) async-start(bf16[8,56,2048]{2,1,0:T(8,128)(2,1)} %copy-done), calls=%async_computation | async-start | bytes 3670016 | tf_op jit(solution)/shard_map/all_to_all | solution.py:265
  29.8 0.0 copy-done.10
  29.8 0.5 collective-permute-start.3
  30.3 0.0 copy-done.11
  30.3 0.1 lt.50
  30.4 0.1 lt.47
  30.5 0.1 lt.48
  30.5 0.1 lt.52
  30.6 0.0 copy-done.9
  30.6 0.0 copy-start.6
  30.6 2.2 %copy-done.6 = bf16[4096,512]{1,0:T(8,128)(2,1)S(1)} copy-done((bf16[4096,512]{1,0:T(8,128)(2,1)S(1)}, bf16[4096,512]{1,0:T(8,128)(2,1)}, u32[]{:S(2)}) %copy-start.6) | copy-done | bytes 4194328
  32.8 2.2 %copy-done.7 = bf16[4096,512]{1,0:T(8,128)(2,1)S(1)} copy-done((bf16[4096,512]{1,0:T(8,128)(2,1)S(1)}, bf16[4096,512]{1,0:T(8,128)(2,1)}, u32[]{:S(2)}) %copy-start.7) | copy-done | bytes 4194328
  35.0 8.8 %project.1 = (bf16[768,512]{1,0:T(8,128)(2,1)S(1)}, bf16[768,512]{1,0:T(8,128)(2,1)S(1)}) custom-call(bf16[768,4096]{1,0:T(8,128)(2,1)} %bitcast.24, bf16[4096,512]{1,0:T(8,128)(2,1)S(1)} %copy-done.6, bf16[4096,512]{1,0:T(8,128)(2,1)S(1)} %copy-done.7, f32[1,128]{1,0:T(1,128)S(1)} %bitcast.23), custom_call_target="tpu_custom_call" | custom-call | flops 6442450944 | bytes 16252928 | tf_op jit(solution)/shard_map/project/pallas_call | solution.py:51
  43.8 0.0 copy-start.1
  43.9 0.9 %copy-done.1 = bf16[768,512]{1,0:T(8,128)(2,1)} copy-done((bf16[768,512]{1,0:T(8,128)(2,1)}, bf16[768,512]{1,0:T(8,128)(2,1)S(1)}, u32[]{:S(2)}) %copy-start.1) | copy-done | bytes 786456
  44.7 0.0 collective-permute-done.3
  44.7 0.1 broadcast_select_fusion.1
  44.8 9.0 %all-to-all-done.rows_ref = bf16[8,56,2048]{2,1,0:T(8,128)(2,1)S(1)} async-done(((bf16[8,56,2048]{2,1,0:T(8,128)(2,1)}), bf16[8,56,2048]{2,1,0:T(8,128)(2,1)S(1)}, u32[]{:S(2)}, u32[]{:S(2)}) %all-to-all-start) | async-done | bytes 1835040 | tf_op jit(solution)/shard_map/all_to_all | solution.py:265
  53.8 0.1 slice.3
  53.9 3.6 %collective-permute-start.4 = (bf16[8,24,2048]{2,1,0:T(8,128)(2,1)S(1)}, bf16[8,24,2048]{2,1,0:T(8,128)(2,1)S(1)}, u32[]{:S(2)}, u32[]{:S(2)}) collective-permute-start(bf16[8,24,2048]{2,1,0:T(8,128)(2,1)S(1)} %slice.3), channel_id=1, source_target_pairs={{0,1},{1,0},{2,3},{3,2},{4,5},{5,4},{6,7},{7,6},{8,9},{9,8},{10,11... | collective-permute-start | bytes 2359304 | tf_op jit(solution)/shard_map/ppermute | solution.py:282
  57.5 1.9 %collective-permute-done.4.bank_ref = bf16[8,24,2048]{2,1,0:T(8,128)(2,1)S(1)} collective-permute-done((bf16[8,24,2048]{2,1,0:T(8,128)(2,1)S(1)}, bf16[8,24,2048]{2,1,0:T(8,128)(2,1)S(1)}, u32[]{:S(2)}, u32[]{:S(2)}) %collective-permute-start.4) | collective-permute-done | bytes 786464 | tf_op jit(solution)/shard_map/ppermute | solution.py:282
  59.4 0.9 %shard_map.102 = bf16[8,16,2048]{2,1,0:T(8,128)(2,1)S(1)} custom-call(bf16[8,56,2048]{2,1,0:T(8,128)(2,1)S(1)} %all-to-all-done.rows_ref, bf16[8,24,2048]{2,1,0:T(8,128)(2,1)S(1)} %collective-permute-done.4.bank_ref), custom_call_target="tpu_custom_call" | custom-call | flops 100663296 | bytes 3145728 | tf_op jit(solution)/shard_map/pallas_call | solution.py:21
  60.3 14.6 %all_to_all.10 = bf16[8,16,2048]{2,1,0:T(8,128)(2,1)S(1)} all-to-all(bf16[8,16,2048]{2,1,0:T(8,128)(2,1)S(1)} %shard_map.102), channel_id=1, replica_groups={{0,16,32,48,64,80,96,112},{2,18,34,50,66,82,98,114},{4,20,36,52,68,84,1..., dimensions={0} | all-to-all | bytes 1048576 | tf_op jit(solution)/shard_map/all_to_all | solution.py:289
  74.9 0.4 unpack.1
  75.3 1.6 %collective-permute-start.5 = (bf16[64,2048]{1,0:T(8,128)(2,1)S(1)}, bf16[64,2048]{1,0:T(8,128)(2,1)S(1)}, u32[]{:S(2)}, u32[]{:S(2)}) collective-permute-start(bf16[64,2048]{1,0:T(8,128)(2,1)S(1)} %get-tuple-element.18), channel_id=1, source_target_pairs={{0,1},{1,0},{2,3},{3,2},{4,5},{5,4},{6,7},{7,6},{8,9},{9,8},{10,11... | collective-permute-start | bytes 786440 | tf_op jit(solution)/shard_map/ppermute | solution.py:306
  76.9 1.2 %collective-permute-done.5.got_ref = bf16[64,2048]{1,0:T(8,128)(2,1)S(1)} collective-permute-done((bf16[64,2048]{1,0:T(8,128)(2,1)S(1)}, bf16[64,2048]{1,0:T(8,128)(2,1)S(1)}, u32[]{:S(2)}, u32[]{:S(2)}) %collective-permute-start.5) | collective-permute-done | bytes 262176 | tf_op jit(solution)/shard_map/ppermute | solution.py:306
  78.1 0.0 copy-done.2
  78.1 1.8 %shard_map.103 = bf16[64,2048]{1,0:T(8,128)(2,1)} custom-call(bf16[64,2048]{1,0:T(8,128)(2,1)S(1)} %get-tuple-element.17.mine_ref, bf16[64,2048]{1,0:T(8,128)(2,1)S(1)} %collective-permute-done.5.got_ref, bf16[64,2048]{1,0:T(8,128)(2,1)S(1)} %pad_maximum_fusion.base_ref, bf16[12,64,512]{2,1,0:T(8,128)(2,1)S(1)} %bitcast.16, ...), custom_call_target="tpu_custom_call" | custom-call | flops 100663296 | bytes 2624512 | tf_op jit(solution)/shard_map/pallas_call | solution.py:21
  (9 shorter events, 0.1 us)
Async XLA Ops:
  0.0 23.3 %collective-permute-start.2 = (bf16[16,2048]{1,0:T(8,128)(2,1)}, bf16[16,2048]{1,0:T(8,128)(2,1)S(1)}, u32[]{:S(2)}, u32[]{:S(2)}) collective-permute-start(bf16[16,2048]{1,0:T(8,128)(2,1)} %bitcast.20), channel_id=1, source_target_pairs={{1,16},{33,48},{65,80},{97,112},{19,2},{51,34},{83,66},{115,98},{5... | collective-permute-start | bytes 196616 | tf_op jit(solution)/shard_map/ppermute | solution.py:251
  5.7 17.6 %collective-permute-start.1 = (bf16[16,4096]{1,0:T(8,128)(2,1)}, bf16[16,4096]{1,0:T(8,128)(2,1)S(1)}, u32[]{:S(2)}, u32[]{:S(2)}) collective-permute-start(bf16[16,4096]{1,0:T(8,128)(2,1)} %bitcast.18), channel_id=1, source_target_pairs={{1,16},{33,48},{65,80},{97,112},{19,2},{51,34},{83,66},{115,98},{5... | collective-permute-start | bytes 393224 | tf_op jit(solution)/shard_map/ppermute | solution.py:250
  7.7 15.9 %collective-permute-start = (bf16[128,2048]{1,0:T(8,128)(2,1)}, bf16[128,2048]{1,0:T(8,128)(2,1)S(1)}, u32[]{:S(2)}, u32[]{:S(2)}) collective-permute-start(bf16[128,2048]{1,0:T(8,128)(2,1)} %mine_ref.1), channel_id=1, source_target_pairs={{0,1},{1,0},{2,3},{3,2},{4,5},{5,4},{6,7},{7,6},{8,9},{9,8},{10,11... | collective-permute-start | bytes 1572872 | tf_op jit(solution)/shard_map/ppermute | solution.py:252
  21.9 0.7 copy-start.8
  22.6 1.0 %copy-start.3 = (bf16[128,2048]{1,0:T(8,128)(2,1)S(1)}, bf16[128,2048]{1,0:T(8,128)(2,1)}, u32[]{:S(2)}) copy-start(bf16[128,2048]{1,0:T(8,128)(2,1)} %mine_ref.1) | copy-start | bytes 1572868
  22.6 1.1 %copy-start.4 = (bf16[1,4096,16]{1,2,0:T(8,128)(2,1)S(1)}, bf16[1,4096,16]{1,2,0:T(8,128)(2,1)}, u32[]{:S(2)}) copy-start(bf16[1,4096,16]{1,2,0:T(8,128)(2,1)} %param.16) | copy-start | bytes 393220
  22.6 1.1 %copy-start.5 = (bf16[1,16,2048]{2,1,0:T(8,128)(2,1)S(1)}, bf16[1,16,2048]{2,1,0:T(8,128)(2,1)}, u32[]{:S(2)}) copy-start(bf16[1,16,2048]{2,1,0:T(8,128)(2,1)} %param.17) | copy-start | bytes 196612
  23.3 6.5 %copy-start.10 = (bf16[128,1024]{1,0:T(8,128)(2,1)S(1)}, bf16[128,1024]{1,0:T(8,128)(2,1)}, u32[]{:S(2)}) copy-start(bf16[128,1024]{1,0:T(8,128)(2,1)} %param.15) | copy-start | bytes 786436
  23.3 7.0 %copy-start.11 = (s32[64]{0:T(128)S(1)}, s32[64]{0:T(128)}, u32[]{:S(2)}) copy-start(s32[64]{0:T(128)} %param.19) | copy-start | bytes 772
  23.3 7.3 %copy-start.9 = (f32[128]{0:T(128)S(1)}, f32[128]{0:T(128)}, u32[]{:S(2)}) copy-start(f32[128]{0:T(128)} %param.13) | copy-start | bytes 1540
  24.7 1.3 %copy-start = (bf16[8,56,2048]{2,1,0:T(8,128)(2,1)}, bf16[8,56,2048]{2,1,0:T(8,128)(2,1)S(1)}, u32[]{:S(2)}) copy-start(bf16[8,56,2048]{2,1,0:T(8,128)(2,1)S(1)} %shard_map.101) | copy-start | bytes 5505028
  26.0 27.8 %all-to-all-start = ((bf16[8,56,2048]{2,1,0:T(8,128)(2,1)}), bf16[8,56,2048]{2,1,0:T(8,128)(2,1)S(1)}, u32[]{:S(2)}, u32[]{:S(2)}) async-start(bf16[8,56,2048]{2,1,0:T(8,128)(2,1)} %copy-done), calls=%async_computation | async-start | bytes 3670016 | tf_op jit(solution)/shard_map/all_to_all | solution.py:265
  29.8 14.9 %collective-permute-start.3 = (bf16[64,1024]{1,0:T(8,128)(2,1)S(1)}, bf16[64,1024]{1,0:T(8,128)(2,1)S(1)}, u32[]{:S(2)}, u32[]{:S(2)}) collective-permute-start(bf16[64,1024]{1,0:T(8,128)(2,1)S(1)} %constant_dynamic-slice_fusion), channel_id=1, source_target_pairs={{0,1},{1,0},{2,3},{3,2},{4,5},{5,4},{6,7},{7,6},{8,9},{9,8},{10,11... | collective-permute-start | bytes 393224 | tf_op jit(solution)/shard_map/ppermute | solution.py:271
  30.6 2.2 %copy-start.6 = (bf16[4096,512]{1,0:T(8,128)(2,1)S(1)}, bf16[4096,512]{1,0:T(8,128)(2,1)}, u32[]{:S(2)}) copy-start(bf16[4096,512]{1,0:T(8,128)(2,1)} %wk_ref.1) | copy-start | bytes 12582916
  32.8 2.2 %copy-start.7 = (bf16[4096,512]{1,0:T(8,128)(2,1)S(1)}, bf16[4096,512]{1,0:T(8,128)(2,1)}, u32[]{:S(2)}) copy-start(bf16[4096,512]{1,0:T(8,128)(2,1)} %wv_ref.1) | copy-start | bytes 12582916
  43.8 0.9 %copy-start.1 = (bf16[768,512]{1,0:T(8,128)(2,1)}, bf16[768,512]{1,0:T(8,128)(2,1)S(1)}, u32[]{:S(2)}) copy-start(bf16[768,512]{1,0:T(8,128)(2,1)S(1)} %get-tuple-element.21) | copy-start | bytes 2359300
  53.8 24.3 %copy-start.2 = (bf16[768,512]{1,0:T(8,128)(2,1)S(1)}, bf16[768,512]{1,0:T(8,128)(2,1)}, u32[]{:S(2)}) copy-start(bf16[768,512]{1,0:T(8,128)(2,1)} %copy-done.1) | copy-start | bytes 2359300
  53.9 5.5 %collective-permute-start.4 = (bf16[8,24,2048]{2,1,0:T(8,128)(2,1)S(1)}, bf16[8,24,2048]{2,1,0:T(8,128)(2,1)S(1)}, u32[]{:S(2)}, u32[]{:S(2)}) collective-permute-start(bf16[8,24,2048]{2,1,0:T(8,128)(2,1)S(1)} %slice.3), channel_id=1, source_target_pairs={{0,1},{1,0},{2,3},{3,2},{4,5},{5,4},{6,7},{7,6},{8,9},{9,8},{10,11... | collective-permute-start | bytes 2359304 | tf_op jit(solution)/shard_map/ppermute | solution.py:282
  75.3 2.8 %collective-permute-start.5 = (bf16[64,2048]{1,0:T(8,128)(2,1)S(1)}, bf16[64,2048]{1,0:T(8,128)(2,1)S(1)}, u32[]{:S(2)}, u32[]{:S(2)}) collective-permute-start(bf16[64,2048]{1,0:T(8,128)(2,1)S(1)} %get-tuple-element.18), channel_id=1, source_target_pairs={{0,1},{1,0},{2,3},{3,2},{4,5},{5,4},{6,7},{7,6},{8,9},{9,8},{10,11... | collective-permute-start | bytes 786440 | tf_op jit(solution)/shard_map/ppermute | solution.py:306

commit v6 on v5

--- a/solution.py
+++ b/solution.py
@@ -10,9 +10,11 @@
 
 TILE_TOKENS = 3
 CHUNK = 16
+FULL = 67043328
 SLOTS = 4
 VMEM = pl.BlockSpec(memory_space=pltpu.VMEM)
 SMEM = pl.BlockSpec(memory_space=pltpu.SMEM)
+HBM = pl.BlockSpec(memory_space=pltpu.HBM)
 
 
 def call(kernel, ins, out, flops, limit=24):
@@ -94,21 +96,29 @@
 
 
 def pack_kernel(
-    side, at_ref, slot_ref, mine_ref, other_ref, down_ref, up_ref, next_down_ref, next_up_ref, out_ref
+    side, at_ref, slot_ref, mine_ref, other_ref, down_ref, up_ref, next_down_ref, next_up_ref, out_ref,
+    placed, piece, sems
 ):
     held = side // 2 * SLOTS
     core, odd, owned = at_ref[0], at_ref[1], at_ref[2]
     width = other_ref.shape[1]
     half = down_ref.shape[0] // 2
+    moves = []
+
+    def send(source, low, high, group):
+        for p in range(side):
+            move = pltpu.make_async_copy(
+                source(p), out_ref.at[p, low:high], sems.at[group * side + p]
+            )
+            move.start()
+            moves.append(move)
 
     def cut(down, up, low):
         rows = slice(low * half, (low + 1) * half)
         left, right = down[rows, :width], down[rows, width:]
-        piece = jnp.concatenate(
-            [jnp.where(core == 0, right, left), jnp.where(core == 0, left, right), up[rows]], axis=0
-        )
-        for p in range(side):
-            out_ref[p, 2 * held :] = piece
+        piece[:half] = jnp.where(core == 0, right, left)
+        piece[half : 2 * half] = jnp.where(core == 0, left, right)
+        piece[2 * half :] = up[rows]
 
     for own, (down, up) in ((1, (down_ref, up_ref)), (0, (next_down_ref, next_up_ref))):
         for low in (0, 1):
@@ -117,13 +127,15 @@
             def _():
                 cut(down, up, low)
 
+    send(lambda p: piece, 2 * held, 2 * held + 3 * half, 2)
     placing = placing_of(slot_ref[:1], side * held)
     for n, source in enumerate((mine_ref, other_ref)):
-        placed = jnp.dot(placing, source[...], preferred_element_type=jnp.float32).astype(
+        placed[n] = jnp.dot(placing, source[...], preferred_element_type=jnp.float32).astype(
             jnp.bfloat16
         )
-        for p in range(side):
-            out_ref[p, n * held : (n + 1) * held] = placed[p * held : (p + 1) * held]
+        send(lambda p: placed.at[n, p * held : (p + 1) * held], n * held, (n + 1) * held, n)
+    for move in moves:
+        move.wait()
 
 
 def raise_kernel(side, rank, rows_ref, bank_ref, out_ref):
@@ -256,12 +268,24 @@
         jax.ShapeDtypeStruct((8, requests), jnp.int32),
         2 * 10**10,
     )
-    packed = call(
+    packed = pl.pallas_call(
         functools.partial(pack_kernel, side),
-        [at, slot, hidden, far_hidden, down, up, next_down, next_up],
-        jax.ShapeDtypeStruct((side, 2 * held + 3 * half, half_model), jnp.bfloat16),
-        4 * side * held * requests * half_model,
-    )
+        out_shape=jax.ShapeDtypeStruct((side, 2 * held + 3 * half, half_model), jnp.bfloat16),
+        in_specs=[SMEM] + [VMEM] * 7,
+        out_specs=HBM,
+        scratch_shapes=[
+            pltpu.VMEM((2, side * held, half_model), jnp.bfloat16),
+            pltpu.VMEM((3 * half, half_model), jnp.bfloat16),
+            pltpu.SemaphoreType.DMA((3 * side,)),
+        ],
+        compiler_params=pltpu.CompilerParams(vmem_limit_bytes=FULL - 12288 * 2**10),
+        cost_estimate=pl.CostEstimate(
+            flops=4 * side * held * requests * half_model,
+            bytes_accessed=4 * hidden.size,
+            transcendentals=0,
+        ),
+        name="pack",
+    )(at, slot, hidden, far_hidden, down, up, next_down, next_up)
     received = lax.all_to_all(packed, both, 0, 0, axis_index_groups=lines, tiled=True)
 
     x = images.transpose(1, 0, 2).reshape(tokens * here, width)

time: 80.3 us -> 80.1 us (level)
  local copies, waits for them, and re-layouts: 7.64 us -> 6.37 us
  Pallas kernels: 13.6 us -> 14.7 us
    pallas_call x0 -> x1, Pallas kernels: none -> 2.07 us  [on_device(): pl.pallas_call(functools.partial(pack_kernel, side), out_shape=jax.ShapeD...]
    unnamed x24, local copies, waits for them, and re-layouts: 7.25 us -> 5.99 us
    pallas_call x4 -> x3, Pallas kernels: 4.38 us -> 3.34 us  [call(): pl.pallas_call(kernel, out_shape=out, in_specs=specs, out_specs=jax.tree....]
where the time goes in v6:
time: 80.1 us; the launch traced here: 79.7 us
  starting transfers between devices  31.4 us (39%)
  Pallas kernels  14.7 us (18%)
  blocking collectives  14.6 us (18%)
  waiting for transfers between devices  12.3 us (15%)
  local copies, waits for them, and re-layouts  6.37 us (8%)
    all_to_all x1, blocking collectives, on_device(): lax.all_to_all(raised, both, 0, 0, axis_index_groups=lines, tiled=True)  14.6 us
    ppermute x1, starting transfers between devices, on_device(): far_hidden = lax.ppermute(hidden, 'ba', swap)  14.2 us
    all_to_all x1, waiting for transfers between devices, on_device(): lax.all_to_all(packed, both, 0, 0, axis_index_groups=lines, tiled=True)  8.94 us
    pallas_call x1, Pallas kernels, project(): pl.pallas_call(functools.partial(project_kernel, kvw // size, size), grid...  8.87 us
    unnamed x24, local copies, waits for them, and re-layouts  5.99 us
    ppermute x1, starting transfers between devices, on_device(): next_up = lax.ppermute(up, both, beside)  5.74 us
    all_to_all x1, starting transfers between devices, on_device(): lax.all_to_all(packed, both, 0, 0, axis_index_groups=lines, tiled=True)  3.81 us
    ppermute x1, starting transfers between devices, on_device(): bank_rows = lax.ppermute(received[:, 2 * held:], 'ba', swap)  3.64 us
  transfers between devices with their start and end apart: 7, of which 4 were waited for; matrix products, arithmetic and copies ran while one was open for 1% of the time, Pallas kernels for 12%

profile of v6, /device:TPU:513, one launch (start us, length us, event | category | flops | bytes accessed | tf_op | source)
XLA Modules:
  0.0 79.7 jit_solution(18395070018134312334)
XLA Ops:
  0.0 5.7 %collective-permute-start.2 = (bf16[16,2048]{1,0:T(8,128)(2,1)}, bf16[16,2048]{1,0:T(8,128)(2,1)S(1)}, u32[]{:S(2)}, u32[]{:S(2)}) collective-permute-start(bf16[16,2048]{1,0:T(8,128)(2,1)} %bitcast.20), channel_id=1, source_target_pairs={{1,16},{33,48},{65,80},{97,112},{19,2},{51,34},{83,66},{115,98},{5... | collective-permute-start | bytes 196616 | tf_op jit(solution)/shard_map/ppermute | solution.py:263
  5.7 2.0 %collective-permute-start.1 = (bf16[16,4096]{1,0:T(8,128)(2,1)}, bf16[16,4096]{1,0:T(8,128)(2,1)S(1)}, u32[]{:S(2)}, u32[]{:S(2)}) collective-permute-start(bf16[16,4096]{1,0:T(8,128)(2,1)} %bitcast.18), channel_id=1, source_target_pairs={{1,16},{33,48},{65,80},{97,112},{19,2},{51,34},{83,66},{115,98},{5... | collective-permute-start | bytes 393224 | tf_op jit(solution)/shard_map/ppermute | solution.py:262
  7.7 14.2 %collective-permute-start = (bf16[128,2048]{1,0:T(8,128)(2,1)}, bf16[128,2048]{1,0:T(8,128)(2,1)S(1)}, u32[]{:S(2)}, u32[]{:S(2)}) collective-permute-start(bf16[128,2048]{1,0:T(8,128)(2,1)} %mine_ref.1), channel_id=1, source_target_pairs={{0,1},{1,0},{2,3},{3,2},{4,5},{5,4},{6,7},{7,6},{8,9},{9,8},{10,11... | collective-permute-start | bytes 1572872 | tf_op jit(solution)/shard_map/ppermute | solution.py:264
  21.9 0.1 pad_add_fusion.at_ref
  21.9 0.0 copy-start.7
  22.0 0.7 copy-done.7
  22.6 0.0 copy-start.2
  22.6 0.0 copy-start.4
  22.6 0.7 shard_map.100.slot_ref
  23.3 0.0 copy-start.9
  23.3 0.0 copy-start.11
  23.3 0.0 copy-start.8
  23.3 0.0 collective-permute-done.2.next_up_ref
  23.3 0.0 collective-permute-done.1.next_down_ref
  23.3 0.3 collective-permute-done.other_ref
  23.6 0.0 copy-done.2
  23.6 0.0 copy-done.3
  23.7 0.0 copy-done.4
  23.7 2.1 %pack.1 = bf16[8,56,2048]{2,1,0:T(8,128)(2,1)} custom-call(s32[3]{0:T(128)S(1)} %pad_add_fusion.at_ref, s32[8,128]{1,0:T(8,128)S(1)} %shard_map.100.slot_ref, bf16[128,2048]{1,0:T(8,128)(2,1)S(1)} %copy-done.2, bf16[128,2048]{1,0:T(8,128)(2,1)S(1)} %collective-permute-done.other_ref, bf16[16,4096]{1,0:T(8,128)(2,1)S(1)} %bitcast.19, ...), custom_call_target="tpu_custom_call" | custom-call | flops 134217728 | bytes 1048576 | tf_op jit(solution)/shard_map/pack/pallas_call | solution.py:271
  25.7 3.8 %all-to-all-start = ((bf16[8,56,2048]{2,1,0:T(8,128)(2,1)}), bf16[8,56,2048]{2,1,0:T(8,128)(2,1)S(1)}, u32[]{:S(2)}, u32[]{:S(2)}) async-start(bf16[8,56,2048]{2,1,0:T(8,128)(2,1)} %pack.1), calls=%async_computation | async-start | bytes 3670016 | tf_op jit(solution)/shard_map/all_to_all | solution.py:289
  29.6 0.0 copy-done.9
  29.6 0.5 collective-permute-start.3
  30.1 0.0 copy-done.11
  30.1 0.1 lt.50
  30.2 0.1 lt.47
  30.2 0.1 lt.48
  30.3 0.1 lt.52
  30.4 0.0 copy-done.8
  30.4 0.0 copy-start.5
  30.4 2.2 %copy-done.5 = bf16[4096,512]{1,0:T(8,128)(2,1)S(1)} copy-done((bf16[4096,512]{1,0:T(8,128)(2,1)S(1)}, bf16[4096,512]{1,0:T(8,128)(2,1)}, u32[]{:S(2)}) %copy-start.5) | copy-done | bytes 4194328
  32.6 2.2 %copy-done.6 = bf16[4096,512]{1,0:T(8,128)(2,1)S(1)} copy-done((bf16[4096,512]{1,0:T(8,128)(2,1)S(1)}, bf16[4096,512]{1,0:T(8,128)(2,1)}, u32[]{:S(2)}) %copy-start.6) | copy-done | bytes 4194328
  34.8 8.9 %project.1 = (bf16[768,512]{1,0:T(8,128)(2,1)S(1)}, bf16[768,512]{1,0:T(8,128)(2,1)S(1)}) custom-call(bf16[768,4096]{1,0:T(8,128)(2,1)} %bitcast.24, bf16[4096,512]{1,0:T(8,128)(2,1)S(1)} %copy-done.5, bf16[4096,512]{1,0:T(8,128)(2,1)S(1)} %copy-done.6, f32[1,128]{1,0:T(1,128)S(1)} %bitcast.23), custom_call_target="tpu_custom_call" | custom-call | flops 6442450944 | bytes 16252928 | tf_op jit(solution)/shard_map/project/pallas_call | solution.py:53
  43.7 0.0 copy-start
  43.7 0.9 %copy-done = bf16[768,512]{1,0:T(8,128)(2,1)} copy-done((bf16[768,512]{1,0:T(8,128)(2,1)}, bf16[768,512]{1,0:T(8,128)(2,1)S(1)}, u32[]{:S(2)}) %copy-start) | copy-done | bytes 786456
  44.6 0.0 collective-permute-done.3
  44.6 0.0 copy-done.10
  44.6 0.1 broadcast_select_fusion.1
  44.7 8.9 %all-to-all-done.rows_ref = bf16[8,56,2048]{2,1,0:T(8,128)(2,1)S(1)} async-done(((bf16[8,56,2048]{2,1,0:T(8,128)(2,1)}), bf16[8,56,2048]{2,1,0:T(8,128)(2,1)S(1)}, u32[]{:S(2)}, u32[]{:S(2)}) %all-to-all-start) | async-done | bytes 1835040 | tf_op jit(solution)/shard_map/all_to_all | solution.py:289
  53.6 0.1 slice.3
  53.7 3.6 %collective-permute-start.4 = (bf16[8,24,2048]{2,1,0:T(8,128)(2,1)S(1)}, bf16[8,24,2048]{2,1,0:T(8,128)(2,1)S(1)}, u32[]{:S(2)}, u32[]{:S(2)}) collective-permute-start(bf16[8,24,2048]{2,1,0:T(8,128)(2,1)S(1)} %slice.3), channel_id=1, source_target_pairs={{0,1},{1,0},{2,3},{3,2},{4,5},{5,4},{6,7},{7,6},{8,9},{9,8},{10,11... | collective-permute-start | bytes 2359304 | tf_op jit(solution)/shard_map/ppermute | solution.py:306
  57.3 1.9 %collective-permute-done.4.bank_ref = bf16[8,24,2048]{2,1,0:T(8,128)(2,1)S(1)} collective-permute-done((bf16[8,24,2048]{2,1,0:T(8,128)(2,1)S(1)}, bf16[8,24,2048]{2,1,0:T(8,128)(2,1)S(1)}, u32[]{:S(2)}, u32[]{:S(2)}) %collective-permute-start.4) | collective-permute-done | bytes 786464 | tf_op jit(solution)/shard_map/ppermute | solution.py:306
  59.2 0.9 %shard_map.101 = bf16[8,16,2048]{2,1,0:T(8,128)(2,1)S(1)} custom-call(bf16[8,56,2048]{2,1,0:T(8,128)(2,1)S(1)} %all-to-all-done.rows_ref, bf16[8,24,2048]{2,1,0:T(8,128)(2,1)S(1)} %collective-permute-done.4.bank_ref), custom_call_target="tpu_custom_call" | custom-call | flops 100663296 | bytes 3145728 | tf_op jit(solution)/shard_map/pallas_call | solution.py:23
  60.1 14.6 %all_to_all.10 = bf16[8,16,2048]{2,1,0:T(8,128)(2,1)S(1)} all-to-all(bf16[8,16,2048]{2,1,0:T(8,128)(2,1)S(1)} %shard_map.101), channel_id=1, replica_groups={{0,16,32,48,64,80,96,112},{2,18,34,50,66,82,98,114},{4,20,36,52,68,84,1..., dimensions={0} | all-to-all | bytes 1048576 | tf_op jit(solution)/shard_map/all_to_all | solution.py:313
  74.7 0.4 unpack.1
  75.1 1.6 %collective-permute-start.5 = (bf16[64,2048]{1,0:T(8,128)(2,1)S(1)}, bf16[64,2048]{1,0:T(8,128)(2,1)S(1)}, u32[]{:S(2)}, u32[]{:S(2)}) collective-permute-start(bf16[64,2048]{1,0:T(8,128)(2,1)S(1)} %get-tuple-element.18), channel_id=1, source_target_pairs={{0,1},{1,0},{2,3},{3,2},{4,5},{5,4},{6,7},{7,6},{8,9},{9,8},{10,11... | collective-permute-start | bytes 786440 | tf_op jit(solution)/shard_map/ppermute | solution.py:330
  76.7 1.2 %collective-permute-done.5.got_ref = bf16[64,2048]{1,0:T(8,128)(2,1)S(1)} collective-permute-done((bf16[64,2048]{1,0:T(8,128)(2,1)S(1)}, bf16[64,2048]{1,0:T(8,128)(2,1)S(1)}, u32[]{:S(2)}, u32[]{:S(2)}) %collective-permute-start.5) | collective-permute-done | bytes 262176 | tf_op jit(solution)/shard_map/ppermute | solution.py:330
  77.9 0.0 copy-done.1
  77.9 1.8 %shard_map.102 = bf16[64,2048]{1,0:T(8,128)(2,1)} custom-call(bf16[64,2048]{1,0:T(8,128)(2,1)S(1)} %get-tuple-element.17.mine_ref, bf16[64,2048]{1,0:T(8,128)(2,1)S(1)} %collective-permute-done.5.got_ref, bf16[64,2048]{1,0:T(8,128)(2,1)S(1)} %pad_maximum_fusion.base_ref, bf16[12,64,512]{2,1,0:T(8,128)(2,1)S(1)} %bitcast.16, ...), custom_call_target="tpu_custom_call" | custom-call | flops 100663296 | bytes 2624512 | tf_op jit(solution)/shard_map/pallas_call | solution.py:23
  (9 shorter events, 0.1 us)
Async XLA Ops:
  0.0 23.3 %collective-permute-start.2 = (bf16[16,2048]{1,0:T(8,128)(2,1)}, bf16[16,2048]{1,0:T(8,128)(2,1)S(1)}, u32[]{:S(2)}, u32[]{:S(2)}) collective-permute-start(bf16[16,2048]{1,0:T(8,128)(2,1)} %bitcast.20), channel_id=1, source_target_pairs={{1,16},{33,48},{65,80},{97,112},{19,2},{51,34},{83,66},{115,98},{5... | collective-permute-start | bytes 196616 | tf_op jit(solution)/shard_map/ppermute | solution.py:263
  5.7 17.6 %collective-permute-start.1 = (bf16[16,4096]{1,0:T(8,128)(2,1)}, bf16[16,4096]{1,0:T(8,128)(2,1)S(1)}, u32[]{:S(2)}, u32[]{:S(2)}) collective-permute-start(bf16[16,4096]{1,0:T(8,128)(2,1)} %bitcast.18), channel_id=1, source_target_pairs={{1,16},{33,48},{65,80},{97,112},{19,2},{51,34},{83,66},{115,98},{5... | collective-permute-start | bytes 393224 | tf_op jit(solution)/shard_map/ppermute | solution.py:262
  7.7 15.9 %collective-permute-start = (bf16[128,2048]{1,0:T(8,128)(2,1)}, bf16[128,2048]{1,0:T(8,128)(2,1)S(1)}, u32[]{:S(2)}, u32[]{:S(2)}) collective-permute-start(bf16[128,2048]{1,0:T(8,128)(2,1)} %mine_ref.1), channel_id=1, source_target_pairs={{0,1},{1,0},{2,3},{3,2},{4,5},{5,4},{6,7},{7,6},{8,9},{9,8},{10,11... | collective-permute-start | bytes 1572872 | tf_op jit(solution)/shard_map/ppermute | solution.py:264
  21.9 0.7 copy-start.7
  22.6 1.0 %copy-start.2 = (bf16[128,2048]{1,0:T(8,128)(2,1)S(1)}, bf16[128,2048]{1,0:T(8,128)(2,1)}, u32[]{:S(2)}) copy-start(bf16[128,2048]{1,0:T(8,128)(2,1)} %mine_ref.1) | copy-start | bytes 1572868
  22.6 1.1 %copy-start.3 = (bf16[1,4096,16]{1,2,0:T(8,128)(2,1)S(1)}, bf16[1,4096,16]{1,2,0:T(8,128)(2,1)}, u32[]{:S(2)}) copy-start(bf16[1,4096,16]{1,2,0:T(8,128)(2,1)} %param.16) | copy-start | bytes 393220
  22.6 1.1 %copy-start.4 = (bf16[1,16,2048]{2,1,0:T(8,128)(2,1)S(1)}, bf16[1,16,2048]{2,1,0:T(8,128)(2,1)}, u32[]{:S(2)}) copy-start(bf16[1,16,2048]{2,1,0:T(8,128)(2,1)} %param.17) | copy-start | bytes 196612
  23.3 6.3 %copy-start.9 = (bf16[128,1024]{1,0:T(8,128)(2,1)S(1)}, bf16[128,1024]{1,0:T(8,128)(2,1)}, u32[]{:S(2)}) copy-start(bf16[128,1024]{1,0:T(8,128)(2,1)} %param.15) | copy-start | bytes 786436
  23.3 6.8 %copy-start.11 = (s32[64]{0:T(128)S(1)}, s32[64]{0:T(128)}, u32[]{:S(2)}) copy-start(s32[64]{0:T(128)} %param.19) | copy-start | bytes 772
  23.3 7.1 %copy-start.8 = (f32[128]{0:T(128)S(1)}, f32[128]{0:T(128)}, u32[]{:S(2)}) copy-start(f32[128]{0:T(128)} %param.13) | copy-start | bytes 1540
  25.7 27.9 %all-to-all-start = ((bf16[8,56,2048]{2,1,0:T(8,128)(2,1)}), bf16[8,56,2048]{2,1,0:T(8,128)(2,1)S(1)}, u32[]{:S(2)}, u32[]{:S(2)}) async-start(bf16[8,56,2048]{2,1,0:T(8,128)(2,1)} %pack.1), calls=%async_computation | async-start | bytes 3670016 | tf_op jit(solution)/shard_map/all_to_all | solution.py:289
  29.6 15.0 %collective-permute-start.3 = (bf16[64,1024]{1,0:T(8,128)(2,1)S(1)}, bf16[64,1024]{1,0:T(8,128)(2,1)S(1)}, u32[]{:S(2)}, u32[]{:S(2)}) collective-permute-start(bf16[64,1024]{1,0:T(8,128)(2,1)S(1)} %constant_dynamic-slice_fusion), channel_id=1, source_target_pairs={{0,1},{1,0},{2,3},{3,2},{4,5},{5,4},{6,7},{7,6},{8,9},{9,8},{10,11... | collective-permute-start | bytes 393224 | tf_op jit(solution)/shard_map/ppermute | solution.py:295
  30.4 2.2 %copy-start.5 = (bf16[4096,512]{1,0:T(8,128)(2,1)S(1)}, bf16[4096,512]{1,0:T(8,128)(2,1)}, u32[]{:S(2)}) copy-start(bf16[4096,512]{1,0:T(8,128)(2,1)} %wk_ref.1) | copy-start | bytes 12582916
  32.6 2.2 %copy-start.6 = (bf16[4096,512]{1,0:T(8,128)(2,1)S(1)}, bf16[4096,512]{1,0:T(8,128)(2,1)}, u32[]{:S(2)}) copy-start(bf16[4096,512]{1,0:T(8,128)(2,1)} %wv_ref.1) | copy-start | bytes 12582916
  34.8 9.8 %copy-start.10 = (bf16[128,1024]{1,0:T(8,128)(2,1)S(1)}, bf16[128,1024]{1,0:T(8,128)(2,1)}, u32[]{:S(2)}) copy-start(bf16[128,1024]{1,0:T(8,128)(2,1)} %param.15) | copy-start | bytes 786436
  43.7 0.9 %copy-start = (bf16[768,512]{1,0:T(8,128)(2,1)}, bf16[768,512]{1,0:T(8,128)(2,1)S(1)}, u32[]{:S(2)}) copy-start(bf16[768,512]{1,0:T(8,128)(2,1)S(1)} %get-tuple-element.21) | copy-start | bytes 2359300
  53.6 24.3 %copy-start.1 = (bf16[768,512]{1,0:T(8,128)(2,1)S(1)}, bf16[768,512]{1,0:T(8,128)(2,1)}, u32[]{:S(2)}) copy-start(bf16[768,512]{1,0:T(8,128)(2,1)} %copy-done) | copy-start | bytes 2359300
  53.7 5.5 %collective-permute-start.4 = (bf16[8,24,2048]{2,1,0:T(8,128)(2,1)S(1)}, bf16[8,24,2048]{2,1,0:T(8,128)(2,1)S(1)}, u32[]{:S(2)}, u32[]{:S(2)}) collective-permute-start(bf16[8,24,2048]{2,1,0:T(8,128)(2,1)S(1)} %slice.3), channel_id=1, source_target_pairs={{0,1},{1,0},{2,3},{3,2},{4,5},{5,4},{6,7},{7,6},{8,9},{9,8},{10,11... | collective-permute-start | bytes 2359304 | tf_op jit(solution)/shard_map/ppermute | solution.py:306
  75.1 2.8 %collective-permute-start.5 = (bf16[64,2048]{1,0:T(8,128)(2,1)S(1)}, bf16[64,2048]{1,0:T(8,128)(2,1)S(1)}, u32[]{:S(2)}, u32[]{:S(2)}) collective-permute-start(bf16[64,2048]{1,0:T(8,128)(2,1)S(1)} %get-tuple-element.18), channel_id=1, source_target_pairs={{0,1},{1,0},{2,3},{3,2},{4,5},{5,4},{6,7},{7,6},{8,9},{9,8},{10,11... | collective-permute-start | bytes 786440 | tf_op jit(solution)/shard_map/ppermute | solution.py:330
